TPU v7x, 32 devices: a whole 2x2x4 slice. The times are simulated.
32 devices in a mesh: img: 2 (over y), sub: 4 (over z), rng: 4 (over x, core).
Axes of the slice: x: 2, y: 2, z: 4, core: 2. Of those that a mesh axis runs over, the one named last changes fastest.
Arguments:
- image: bfloat16 [2, 16, 128, 4096], P(None, ('img', 'sub'), None, 'rng'), parts along dimension 1, may hold values from -6 to 6
- interp_weights: bfloat16 [4, 2, 2, 2, 128, 128], replicated, may hold values from -0.25 to 0.25
- range_taps: float32 [4, 4], replicated, may hold values from -2 to 2
- range_shifts: int32 [4, 2, 128], replicated, may hold values from -8 to 5
Outputs:
- merged_image: bfloat16 [2, 16, 128, 4096], P(None, ('img', 'sub'), None, 'rng'), parts along dimension 1
There are 2 independent parts, one for each index of `img`. A program takes and returns all parts, laid end to end along the dimension named above; an argument that names none is the same for every part. Nothing has to cross between parts.
All inputs are finite; a program needn't handle non-finite values.
Results may differ from a plain program's by a relative error of at most 0.0095.
Values may be sent and summed in bfloat16 or wider, within the bound.
A program may use at most 64 MiB of HBM per device.

v0:
```python
import math

import functools

import jax
import jax.numpy as jnp
import numpy as np
from jax import lax
from jax.experimental import pallas as pl
from jax.experimental.pallas import tpu as pltpu
from jax.sharding import PartitionSpec as P

ANGLES = 128
RANGE = 4096
RIM = 8
TAPS = 4
LEVELS = 4


phase_step = 2.0 * math.pi / 64.0


def padded_2(cells, sides, width):
    for axis, dim in sides:
        count = lax.axis_size(axis)
        ends = count - 1
        head = lax.slice_in_dim(cells, 0, width, axis=dim)
        tail = lax.slice_in_dim(cells, cells.shape[dim] - width, cells.shape[dim], axis=dim)
        cells = jnp.concatenate(
            [
                lax.ppermute(tail, axis, [(i, (i + 1) % count) for i in range(ends)]),
                cells,
                lax.ppermute(head, axis, [((i + 1) % count, i) for i in range(ends)]),
            ],
            axis=dim,
        )
    return cells


def from_partner(value, axis, stride):
    mask = 2**stride
    pairs = [(source, source ^ mask) for source in range(lax.axis_size(axis))]
    return lax.ppermute(value, axis, pairs)


def rotate(merged_sum, level_index, half_index, range_start, range_width):
    angle_rows = half_index * ANGLES + jnp.arange(ANGLES, dtype=jnp.int32)
    range_cols = range_start + jnp.arange(range_width, dtype=jnp.int32)
    wrapped = range_cols[None, :] * (angle_rows[:, None] + 1) * (7 + level_index) % 64
    phase = wrapped.astype(jnp.float32) * phase_step
    cosine = jnp.cos(phase)
    sinus = jnp.sin(phase)
    return jnp.stack(
        [
            merged_sum[0] * cosine - merged_sum[1] * sinus,
            merged_sum[0] * sinus + merged_sum[1] * cosine,
        ]
    )


def level_coef(range_taps, range_shifts, level_index, side_index):
    offsets = jnp.arange(2 * RIM + 1, dtype=jnp.int32) - RIM
    tap_ids = jnp.arange(TAPS, dtype=jnp.int32)
    hits = (
        range_shifts[level_index, side_index][:, None, None] + tap_ids[None, :, None]
        == offsets[None, None, :]
    )
    return jnp.einsum(
        "t,ato->ao",
        range_taps[level_index],
        hits.astype(jnp.float32),
        precision=lax.Precision.HIGHEST,
    )


def interpolate(padded, coef, range_width):
    total = None
    for offset_index in range(2 * RIM + 1):
        term = coef[:, offset_index, None] * padded[
            ..., offset_index : offset_index + range_width
        ].astype(jnp.float32)
        total = term if total is None else total + term
    return total.astype(jnp.bfloat16)


def block_of(weight_pair):
    return jnp.stack(
        [jnp.stack([weight_pair[0], -weight_pair[1]]), jnp.stack([weight_pair[1], weight_pair[0]])]
    )


def combine_sides(lower_rows, upper_rows, weights_level, half_index):
    chosen = lax.dynamic_index_in_dim(weights_level, half_index, 1, keepdims=False)
    merged_sum = None
    for side_index, source in ((0, lower_rows), (1, upper_rows)):
        product = jnp.einsum(
            "xcij,cgjr->xgir",
            block_of(chosen[side_index]),
            source,
            preferred_element_type=jnp.float32,
        )
        merged_sum = product if merged_sum is None else merged_sum + product
    return merged_sum


def on_device(image, interp_weights, range_taps, range_shifts):
    range_width = image.shape[3]
    sub_count = lax.axis_size("sub")
    bit_count = sub_count.bit_length() - 1
    sub_index = lax.axis_index("sub")
    range_start = lax.axis_index("rng") * range_width
    current = padded_2(image, (("rng", 3),), LEVELS * RIM)
    margin = LEVELS * RIM
    for level_index in range(LEVELS):
        bit = level_index % bit_count
        own_half = sub_index // 2**bit % 2
        padded = current
        margin = margin - RIM
        out_width = range_width + 2 * margin
        coef = jnp.where(
            own_half == 0,
            level_coef(range_taps, range_shifts, level_index, 0),
            level_coef(range_taps, range_shifts, level_index, 1),
        )
        own_rows = interpolate(padded, coef, out_width)
        partner = from_partner(own_rows, "sub", bit)
        lower_rows = jnp.where(own_half == 0, own_rows, partner)
        upper_rows = jnp.where(own_half == 0, partner, own_rows)
        merged = combine_sides(lower_rows, upper_rows, interp_weights[level_index], own_half)
        turned = rotate(merged, level_index, own_half, range_start - margin, out_width)
        global_cols = range_start - margin + jnp.arange(out_width, dtype=jnp.int32)
        inside = jnp.logical_and(global_cols >= 0, global_cols < RANGE)
        turned = jnp.where(inside, turned, 0.0)
        current = turned.astype(jnp.bfloat16)
    return current


PERIOD = 64
LANES = 128
HALO = LEVELS * RIM
MESH = pl.DeviceIdType.MESH
NT = (((1,), (1,)), ((), ()))


def phase_tables():
    a = np.arange(ANGLES)
    tables = np.zeros((LEVELS, 2, 2, PERIOD, ANGLES), np.float32)
    for level in range(LEVELS):
        for half in range(2):
            start = -HALO if level < LEVELS - 1 else 0
            r = (start + np.arange(PERIOD))[:, None]
            wrapped = (r * (half * ANGLES + a + 1)[None, :] * (7 + level)) % PERIOD
            phase = wrapped * phase_step
            tables[level, half, 0] = np.cos(phase)
            tables[level, half, 1] = np.sin(phase)
    last = np.swapaxes(tables[LEVELS - 1], -1, -2)
    last = np.concatenate([last] * (LANES // PERIOD), -1)
    return tables[: LEVELS - 1], last


def merge_kernel(
    n, rngs, image_hbm, weights_hbm, taps, shifts, rows_hbm, cols_hbm, out,
    image, weights, rows_table, cols_table, load_sem,
    xt, xin, big, table, xf, sh0, sh1, sh2, ybuf, stage,
    in_send, in_recv, left_send, left_recv, right_send, right_recv, twin_send, twin_recv, out_send, out_recv,
):
    me = lax.axis_index("sub")
    place = lax.axis_index("rng")
    groups, width = image_hbm.shape[1], image_hbm.shape[3]
    block = width // n
    rows = block + 2 * HALO
    bits = n.bit_length() - 1

    twin = place % 2
    first = place - twin
    mine = 2 * me + twin
    near = (HALO, 0), (0, HALO)

    def span(b):
        start = b % n * block
        lo = max(start - near[b % 2][0], 0)
        hi = min(start + block + near[b % 2][1], width)
        return lo, HALO + lo - start, hi - lo

    def in_copy(g, src, b):
        lo, off, size = span(b)
        return pltpu.make_async_remote_copy(
            src_ref=xt.at[g, :, pl.ds(lo, size), :],
            dst_ref=xin.at[g, src, :, pl.ds(off, size), :],
            send_sem=in_send.at[g, b],
            recv_sem=in_recv.at[g, src],
            device_id={"sub": b // 2, "rng": first + b % 2},
            device_id_type=MESH,
        )

    def twin_copy(g, size_from, size_to):
        return pltpu.make_async_remote_copy(
            src_ref=xin.at[g, :, :, pl.ds(size_from, HALO), :],
            dst_ref=xin.at[g, :, :, pl.ds(size_to, HALO), :],
            send_sem=twin_send.at[g],
            recv_sem=twin_recv.at[g],
            device_id={"rng": place + 1 - 2 * twin},
            device_id_type=MESH,
        )

    def left_copy(g, src):
        return pltpu.make_async_remote_copy(
            src_ref=xt.at[g, :, pl.ds(width - HALO, HALO), :],
            dst_ref=xin.at[g, src, :, pl.ds(0, HALO), :],
            send_sem=left_send.at[g],
            recv_sem=left_recv.at[g, src],
            device_id={"sub": (1 - twin) * (n // 2), "rng": first + 2 * twin},
            device_id_type=MESH,
        )

    def right_copy(g, src):
        return pltpu.make_async_remote_copy(
            src_ref=xt.at[g, :, pl.ds(0, HALO), :],
            dst_ref=xin.at[g, src, :, pl.ds(rows - HALO, HALO), :],
            send_sem=right_send.at[g],
            recv_sem=right_recv.at[g, src],
            device_id={"sub": twin * (n // 2) + (1 - twin) * n - 1, "rng": first - 1 + 2 * twin},
            device_id_type=MESH,
        )

    def out_copy(g, z, owner):
        return pltpu.make_async_remote_copy(
            src_ref=stage.at[g, z],
            dst_ref=out.at[:, g, :, pl.ds(pl.multiple_of(owner % n * block, LANES), block)],
            send_sem=out_send.at[g, z],
            recv_sem=out_recv.at[g, owner % n],
            device_id={"sub": z, "rng": first + owner // n},
            device_id_type=MESH,
        )

    left_self = jnp.logical_and(twin == 0, me == n // 2)
    left_out = jnp.logical_and(jnp.logical_not(left_self), place < rngs - 1)
    right_self = jnp.logical_and(twin == 1, me == n // 2 - 1)
    right_out = jnp.logical_and(jnp.logical_not(right_self), place > 0)

    head_from_left = jnp.logical_and(mine == 0, place > 0)
    tail_from_right = jnp.logical_and(mine == 2 * n - 1, place < rngs - 1)
    barrier = pltpu.get_barrier_semaphore()

    def ready(cond, z, r):
        @pl.when(cond)
        def _():
            pl.semaphore_signal(
                barrier, inc=1, device_id={"sub": z, "rng": r}, device_id_type=MESH
            )

    for z in range(n):
        for c in range(2):
            ready(mine != 2 * z + c, z, first + c)
        ready(head_from_left, z, place - 1)
        ready(tail_from_right, z, place + 1)

    loads = [
        pltpu.make_async_copy(image_hbm.at[:, g], image.at[:, g], load_sem.at[g])
        for g in range(groups)
    ]
    others = [
        pltpu.make_async_copy(src, dst, load_sem.at[groups + k])
        for k, (src, dst) in enumerate(
            ((weights_hbm, weights), (rows_hbm, rows_table), (cols_hbm, cols_table))
        )
    ]
    for copy in loads + others:
        copy.start()

    eye = (
        lax.broadcasted_iota(jnp.int32, (LANES, LANES), 0)
        == lax.broadcasted_iota(jnp.int32, (LANES, LANES), 1)
    ).astype(jnp.bfloat16)

    for g in range(groups):
        loads[g].wait()
        for c in range(2):
            for k in range(width // LANES):
                cols = pl.ds(k * LANES, LANES)
                xt[g, c, cols, :] = lax.dot_general(
                    eye, image[c, g, :, cols], NT, preferred_element_type=jnp.float32
                ).astype(jnp.bfloat16)
        if g == 0:
            sends_edge = jnp.where(twin == 1, place < rngs - 1, place > 0)
            pl.semaphore_wait(barrier, 2 * n - 1 + sends_edge.astype(jnp.int32))

        @pl.when(left_out)
        def _():
            left_copy(g, me).start()

        @pl.when(right_out)
        def _():
            right_copy(g, me).start()

        for b in range(2 * n):

            @pl.when(jnp.logical_and(twin == b // n, mine != b))
            def _():
                in_copy(g, me, b).start()

    at_left = jnp.logical_and(place == 0, me == 0)
    at_right = jnp.logical_and(place == rngs - 1, me == n - 1)

    for b in range(2 * n):
        z = b // 2
        if b % 2 == b // n:

            @pl.when(mine == b)
            def _():
                lo, off, size = span(b)
                for g in range(groups):
                    xin[g, z, :, off : off + size, :] = xt[g, :, lo : lo + size, :]

    @pl.when(left_self)
    def _():
        for g in range(groups):
            xin[g, n // 2, :, :HALO, :] = xt[g, :, width - HALO :, :]

    @pl.when(right_self)
    def _():
        for g in range(groups):
            xin[g, n // 2 - 1, :, rows - HALO :, :] = xt[g, :, :HALO, :]

    @pl.when(at_left)
    def _():
        xin[:, :, :, :HALO, :] = jnp.zeros((groups, n, 2, HALO, ANGLES), jnp.bfloat16)

    @pl.when(at_right)
    def _():
        xin[:, :, :, rows - HALO :, :] = jnp.zeros((groups, n, 2, HALO, ANGLES), jnp.bfloat16)

    for copy in others:
        copy.wait()

    for level in range(LEVELS):
        for half in range(2):
            for side in range(2):
                real = weights[level, side, half, 0]
                imag = weights[level, side, half, 1]
                i = half * 2 * ANGLES
                j = side * 2 * ANGLES
                big[level, i : i + ANGLES, j : j + ANGLES] = real
                big[level, i : i + ANGLES, j + ANGLES : j + 2 * ANGLES] = -imag
                big[level, i + ANGLES : i + 2 * ANGLES, j : j + ANGLES] = imag
                big[level, i + ANGLES : i + 2 * ANGLES, j + ANGLES : j + 2 * ANGLES] = real
            if level < LEVELS - 1:
                for part in range(2):
                    for start in range(0, rows, PERIOD):
                        size = min(PERIOD, rows - start)
                        table[level, half, part, start : start + size, :] = rows_table[
                            level, half, part, :size, :
                        ]

    def send_back(g, s):
        here = jnp.logical_and(s == me, twin == mine // n)

        @pl.when(jnp.logical_not(here))
        def _():
            out_copy(g, s, mine).start()

        @pl.when(here)
        def _():
            out[:, g, :, pl.ds(pl.multiple_of(mine % n * block, LANES), block)] = stage[g, s]

    def per_group(g, carry):
        for b in range(2 * n):

            @pl.when(mine == b)
            def _():
                for src in range(n):
                    if b % 2 != b // n or src != b // 2:
                        in_copy(g, src, b).wait_recv()
                if b % 2 == 0:
                    twin_copy(g, block, 0).start()
                else:
                    twin_copy(g, HALO, rows - HALO).start()

        @pl.when(jnp.logical_or(mine == n, jnp.logical_and(mine == 0, place > 0)))
        def _():
            for src in range(n):

                @pl.when(jnp.logical_or(mine == 0, src != n // 2))
                def _():
                    left_copy(g, src).wait_recv()

        @pl.when(jnp.logical_or(mine == n - 1, jnp.logical_and(mine == 2 * n - 1, place < rngs - 1)))
        def _():
            for src in range(n):

                @pl.when(jnp.logical_or(mine == 2 * n - 1, src != n // 2 - 1))
                def _():
                    right_copy(g, src).wait_recv()

        twin_copy(g, 0, 0).wait()

        for s in range(n):
            for c in range(2):
                xf[s, c, :rows, :] = xin[g, s, c].astype(jnp.float32)

        for level in range(LEVELS):
            mask = 2 ** (level % bits)
            base = RIM * level
            count = rows - 2 * base
            kept = count - 2 * RIM
            wide = kept + RIM

            def per_pair(pair, inner, level=level, mask=mask, base=base, count=count, kept=kept, wide=wide):
                low = pair // mask * (2 * mask) + pair % mask
                members = (low, low + mask)
                for side in range(2):
                    k = shifts[level, side][None, :] + RIM
                    on8, on4, on2, on1 = [(k // p) % 2 == 1 for p in (8, 4, 2, 1)]
                    for c in range(2):
                        s = members[side]
                        u = None
                        for t in range(TAPS):
                            term = taps[level, t] * xf[s, c, pl.ds(base + t, count), :]
                            u = term if u is None else u + term
                        v = jnp.where(on8, u[RIM:], u[:wide])
                        sh0[:wide] = v
                        v = jnp.where(on4, sh0[pl.ds(4, wide), :], v)
                        sh1[:wide] = v
                        v = jnp.where(on2, sh1[pl.ds(2, wide), :], v)
                        sh2[:wide] = v
                        v = jnp.where(on1, sh2[pl.ds(1, kept), :], v[:kept])
                        j = (side * 2 + c) * ANGLES
                        ybuf[:kept, j : j + ANGLES] = v.astype(jnp.bfloat16)
                y = ybuf[:kept, :]
                if level < LEVELS - 1:
                    z = lax.dot_general(y, big[level], NT, preferred_element_type=jnp.float32)
                    for half in range(2):
                        s = members[half]
                        j = half * 2 * ANGLES
                        re, im = z[:, j : j + ANGLES], z[:, j + ANGLES : j + 2 * ANGLES]
                        span_rows = pl.ds(base + RIM, kept)
                        cosine = table[level, half, 0, span_rows, :]
                        sinus = table[level, half, 1, span_rows, :]
                        xf[s, 0, span_rows, :] = re * cosine - im * sinus
                        xf[s, 1, span_rows, :] = re * sinus + im * cosine
                else:
                    z = lax.dot_general(big[level], y, NT, preferred_element_type=jnp.float32)
                    for half in range(2):
                        s = members[half]
                        i = half * 2 * ANGLES
                        cosine, sinus = cols_table[half, 0], cols_table[half, 1]
                        for start in range(0, block, LANES):
                            cols = slice(start, start + LANES)
                            re, im = z[i : i + ANGLES, cols], z[i + ANGLES : i + 2 * ANGLES, cols]
                            stage[g, s, 0, :, cols] = (re * cosine - im * sinus).astype(jnp.bfloat16)
                            stage[g, s, 1, :, cols] = (re * sinus + im * cosine).astype(jnp.bfloat16)
                    for half in range(2):
                        send_back(g, members[half])

                return inner

            lax.fori_loop(0, n // 2, per_pair, 0)
            if level < LEVELS - 1:

                @pl.when(at_left)
                def _():
                    xf[:, :, :HALO, :] = jnp.zeros((n, 2, HALO, ANGLES), jnp.float32)

                @pl.when(at_right)
                def _():
                    xf[:, :, rows - HALO : rows, :] = jnp.zeros((n, 2, HALO, ANGLES), jnp.float32)

        return carry

    lax.fori_loop(0, groups, per_group, 0)

    for g in range(groups):
        for b in range(2 * n):

            @pl.when(jnp.logical_and(twin == b // n, mine != b))
            def _():
                in_copy(g, me, b).wait_send()

        for z in range(n):

            @pl.when(jnp.logical_not(jnp.logical_and(me == z, twin == mine // n)))
            def _():
                out_copy(g, z, mine).wait_send()

            @pl.when(mine != n * twin + z)
            def _():
                out_copy(g, z, n * twin + z).wait_recv()

        @pl.when(left_out)
        def _():
            left_copy(g, me).wait_send()

        @pl.when(right_out)
        def _():
            right_copy(g, me).wait_send()


def in_one_kernel(n, rngs, image, interp_weights, range_taps, range_shifts):
    groups, width = image.shape[1], image.shape[3]
    block = width // n
    rows = block + 2 * HALO
    rows_table, cols_table = phase_tables()
    vmem = pl.BlockSpec(memory_space=pltpu.VMEM)
    hbm = pl.BlockSpec(memory_space=pl.ANY)
    dma = pltpu.SemaphoreType.DMA
    f32, bf16 = jnp.float32, jnp.bfloat16
    return pl.pallas_call(
        functools.partial(merge_kernel, n, rngs),
        out_shape=jax.ShapeDtypeStruct(image.shape, bf16),
        in_specs=[hbm, hbm, pl.BlockSpec(memory_space=pltpu.SMEM), vmem, hbm, hbm],
        out_specs=vmem,
        scratch_shapes=[
            pltpu.VMEM(image.shape, bf16),
            pltpu.VMEM(interp_weights.shape, bf16),
            pltpu.VMEM(rows_table.shape, f32),
            pltpu.VMEM(cols_table.shape, f32),
            dma((groups + 3,)),
            pltpu.VMEM((groups, 2, width, ANGLES), bf16),
            pltpu.VMEM((groups, n, 2, rows, ANGLES), bf16),
            pltpu.VMEM((LEVELS, 4 * ANGLES, 4 * ANGLES), bf16),
            pltpu.VMEM((LEVELS - 1, 2, 2, rows, ANGLES), f32),
            pltpu.VMEM((n, 2, rows + 8, ANGLES), f32),
            pltpu.VMEM((rows + 8, ANGLES), f32),
            pltpu.VMEM((rows + 8, ANGLES), f32),
            pltpu.VMEM((rows + 8, ANGLES), f32),
            pltpu.VMEM((rows, 4 * ANGLES), bf16),
            pltpu.VMEM((groups, n, 2, ANGLES, block), bf16),
            dma((groups, 2 * n)),
            dma((groups, n)),
            dma((groups,)),
            dma((groups, n)),
            dma((groups,)),
            dma((groups, n)),
            dma((groups,)),
            dma((groups,)),
            dma((groups, n)),
            dma((groups, n)),
        ],
        compiler_params=pltpu.CompilerParams(has_side_effects=True, collective_id=0),
    )(image, interp_weights, range_taps, range_shifts, rows_table, cols_table)


def fits_kernel(mesh, width):
    n = mesh.shape["sub"]
    block = width // n
    paired = mesh.shape["rng"] % 2 == 0
    return paired and n > 1 and n & (n - 1) == 0 and block % LANES == 0 and block >= HALO and ANGLES == LANES


def per_device(mesh, image, *rest):
    if fits_kernel(mesh, image.shape[3]):
        return in_one_kernel(mesh.shape["sub"], mesh.shape["rng"], image, *rest)
    return on_device(image, *rest)


def solution(mesh):
    return jax.shard_map(
        functools.partial(per_device, mesh),
        mesh=mesh,
        in_specs=(P(None, ("img", "sub"), None, "rng"), P(), P(), P()),
        out_specs=P(None, ("img", "sub"), None, "rng"),
        check_vma=False,
    )
```

profile of v0, /device:TPU:15, one launch (start us, length us, event | category | flops | bytes accessed | tf_op | source)
XLA Modules:
  0.0 59.6 jit_solution(11071727029183447400)
XLA Ops:
  0.0 57.3 %shard_map.64 = bf16[2,2,128,1024]{3,2,1,0:T(8,128)(2,1)} custom-call(bf16[2,2,128,1024]{3,2,1,0:T(8,128)(2,1)} %image_hbm.1, bf16[4,2,2,2,128,128]{5,4,3,2,1,0:T(8,128)(2,1)} %weights_hbm.1, f32[4,4]{1,0:T(4,128)} %taps.1, s32[4,2,128]{2,1,0:T(2,128)} %shifts.1, f32[3,2,2,64,128]{4,3,2,1,0:T(8,128)} %constant.4.clone.rows_hbm, ...), custom_call_target="tpu_custom_call" | custom-call | tf_op jit(solution)/shard_map/pallas_call | solution.py:507
  57.3 2.3 %copy.8 = bf16[2,2,128,1024]{3,2,1,0:T(8,128)(2,1)} copy(bf16[2,2,128,1024]{3,2,1,0:T(8,128)(2,1)} %shard_map.64) | data formatting | bytes 2097152
where the time goes:
time: 59.7 us; the launch traced here: 59.6 us
  Pallas kernels  57.3 us (96%)
  local copies, waits for them, and re-layouts  2.26 us (4%)
    pallas_call x1, Pallas kernels, in_one_kernel(): pl.pallas_call(functools.partial(merge_kernel, n, rngs), out_shape=jax.Sh...  57.3 us
    unnamed x1, local copies, waits for them, and re-layouts  2.26 us

commit v1 on v0

--- a/solution.py
+++ b/solution.py
@@ -506,7 +506,7 @@
     f32, bf16 = jnp.float32, jnp.bfloat16
     return pl.pallas_call(
         functools.partial(merge_kernel, n, rngs),
-        out_shape=jax.ShapeDtypeStruct(image.shape, bf16),
+        out_shape=pltpu.VMEM(image.shape, bf16),
         in_specs=[hbm, hbm, pl.BlockSpec(memory_space=pltpu.SMEM), vmem, hbm, hbm],
         out_specs=vmem,
         scratch_shapes=[

time: 59.7 us -> 57.5 us (0.963)
  local copies, waits for them, and re-layouts: 2.26 us -> 0.97 us
  Pallas kernels: 57.3 us -> 56.3 us
    unnamed x1, local copies, waits for them, and re-layouts: 2.26 us -> 0.97 us
    pallas_call x1, Pallas kernels: 57.3 us -> 56.3 us  [in_one_kernel(): pl.pallas_call(functools.partial(merge_kernel, n, rngs), out_shape=pltpu....]
where the time goes in v1:
time: 57.5 us; the launch traced here: 57.3 us
  Pallas kernels  56.3 us (98%)
  local copies, waits for them, and re-layouts  0.97 us (2%)
    pallas_call x1, Pallas kernels, in_one_kernel(): pl.pallas_call(functools.partial(merge_kernel, n, rngs), out_shape=pltpu....  56.3 us

profile of v1, /device:TPU:15, one launch (start us, length us, event | category | flops | bytes accessed | tf_op | source)
XLA Modules:
  0.0 57.3 jit_solution(6545520232210470124)
XLA Ops:
  0.0 56.3 %shard_map.64 = bf16[2,2,128,1024]{3,2,1,0:T(8,128)(2,1)S(1)} custom-call(bf16[2,2,128,1024]{3,2,1,0:T(8,128)(2,1)} %image_hbm.1, bf16[4,2,2,2,128,128]{5,4,3,2,1,0:T(8,128)(2,1)} %weights_hbm.1, f32[4,4]{1,0:T(4,128)} %taps.1, s32[4,2,128]{2,1,0:T(2,128)} %shifts.1, f32[3,2,2,64,128]{4,3,2,1,0:T(8,128)} %constant.4.clone.rows_hbm, ...), custom_call_target="tpu_custom_call" | custom-call | tf_op jit(solution)/shard_map/pallas_call | solution.py:507
  56.3 1.0 %copy.8 = bf16[2,2,128,1024]{3,2,1,0:T(8,128)(2,1)} copy(bf16[2,2,128,1024]{3,2,1,0:T(8,128)(2,1)S(1)} %shard_map.64) | data formatting | bytes 2097152

commit v2 on v1

v2 whole, which is shorter than its diff:
```python
import math

import functools

import jax
import jax.numpy as jnp
import numpy as np
from jax import lax
from jax.experimental import pallas as pl
from jax.experimental.pallas import tpu as pltpu
from jax.sharding import PartitionSpec as P

ANGLES = 128
RANGE = 4096
RIM = 8
TAPS = 4
LEVELS = 4


phase_step = 2.0 * math.pi / 64.0


def padded_2(cells, sides, width):
    for axis, dim in sides:
        count = lax.axis_size(axis)
        ends = count - 1
        head = lax.slice_in_dim(cells, 0, width, axis=dim)
        tail = lax.slice_in_dim(cells, cells.shape[dim] - width, cells.shape[dim], axis=dim)
        cells = jnp.concatenate(
            [
                lax.ppermute(tail, axis, [(i, (i + 1) % count) for i in range(ends)]),
                cells,
                lax.ppermute(head, axis, [((i + 1) % count, i) for i in range(ends)]),
            ],
            axis=dim,
        )
    return cells


def from_partner(value, axis, stride):
    mask = 2**stride
    pairs = [(source, source ^ mask) for source in range(lax.axis_size(axis))]
    return lax.ppermute(value, axis, pairs)


def rotate(merged_sum, level_index, half_index, range_start, range_width):
    angle_rows = half_index * ANGLES + jnp.arange(ANGLES, dtype=jnp.int32)
    range_cols = range_start + jnp.arange(range_width, dtype=jnp.int32)
    wrapped = range_cols[None, :] * (angle_rows[:, None] + 1) * (7 + level_index) % 64
    phase = wrapped.astype(jnp.float32) * phase_step
    cosine = jnp.cos(phase)
    sinus = jnp.sin(phase)
    return jnp.stack(
        [
            merged_sum[0] * cosine - merged_sum[1] * sinus,
            merged_sum[0] * sinus + merged_sum[1] * cosine,
        ]
    )


def level_coef(range_taps, range_shifts, level_index, side_index):
    offsets = jnp.arange(2 * RIM + 1, dtype=jnp.int32) - RIM
    tap_ids = jnp.arange(TAPS, dtype=jnp.int32)
    hits = (
        range_shifts[level_index, side_index][:, None, None] + tap_ids[None, :, None]
        == offsets[None, None, :]
    )
    return jnp.einsum(
        "t,ato->ao",
        range_taps[level_index],
        hits.astype(jnp.float32),
        precision=lax.Precision.HIGHEST,
    )


def interpolate(padded, coef, range_width):
    total = None
    for offset_index in range(2 * RIM + 1):
        term = coef[:, offset_index, None] * padded[
            ..., offset_index : offset_index + range_width
        ].astype(jnp.float32)
        total = term if total is None else total + term
    return total.astype(jnp.bfloat16)


def block_of(weight_pair):
    return jnp.stack(
        [jnp.stack([weight_pair[0], -weight_pair[1]]), jnp.stack([weight_pair[1], weight_pair[0]])]
    )


def combine_sides(lower_rows, upper_rows, weights_level, half_index):
    chosen = lax.dynamic_index_in_dim(weights_level, half_index, 1, keepdims=False)
    merged_sum = None
    for side_index, source in ((0, lower_rows), (1, upper_rows)):
        product = jnp.einsum(
            "xcij,cgjr->xgir",
            block_of(chosen[side_index]),
            source,
            preferred_element_type=jnp.float32,
        )
        merged_sum = product if merged_sum is None else merged_sum + product
    return merged_sum


def on_device(image, interp_weights, range_taps, range_shifts):
    range_width = image.shape[3]
    sub_count = lax.axis_size("sub")
    bit_count = sub_count.bit_length() - 1
    sub_index = lax.axis_index("sub")
    range_start = lax.axis_index("rng") * range_width
    current = padded_2(image, (("rng", 3),), LEVELS * RIM)
    margin = LEVELS * RIM
    for level_index in range(LEVELS):
        bit = level_index % bit_count
        own_half = sub_index // 2**bit % 2
        padded = current
        margin = margin - RIM
        out_width = range_width + 2 * margin
        coef = jnp.where(
            own_half == 0,
            level_coef(range_taps, range_shifts, level_index, 0),
            level_coef(range_taps, range_shifts, level_index, 1),
        )
        own_rows = interpolate(padded, coef, out_width)
        partner = from_partner(own_rows, "sub", bit)
        lower_rows = jnp.where(own_half == 0, own_rows, partner)
        upper_rows = jnp.where(own_half == 0, partner, own_rows)
        merged = combine_sides(lower_rows, upper_rows, interp_weights[level_index], own_half)
        turned = rotate(merged, level_index, own_half, range_start - margin, out_width)
        global_cols = range_start - margin + jnp.arange(out_width, dtype=jnp.int32)
        inside = jnp.logical_and(global_cols >= 0, global_cols < RANGE)
        turned = jnp.where(inside, turned, 0.0)
        current = turned.astype(jnp.bfloat16)
    return current


PERIOD = 64
LANES = 128
CORES = 2
HALO = LEVELS * RIM
MESH = pl.DeviceIdType.MESH
NT = (((1,), (1,)), ((), ()))


def phase_tables():
    a = np.arange(ANGLES)
    tables = np.zeros((LEVELS, 2, 2, PERIOD, ANGLES), np.float32)
    for level in range(LEVELS):
        for half in range(2):
            start = -HALO if level < LEVELS - 1 else 0
            r = (start + np.arange(PERIOD))[:, None]
            wrapped = (r * (half * ANGLES + a + 1)[None, :] * (7 + level)) % PERIOD
            phase = wrapped * phase_step
            tables[level, half, 0] = np.cos(phase)
            tables[level, half, 1] = np.sin(phase)
    last = np.swapaxes(tables[LEVELS - 1], -1, -2)
    last = np.concatenate([last] * (LANES // PERIOD), -1)
    return tables[: LEVELS - 1], last


def merge_kernel(
    n, rngs, image_hbm, weights_hbm, taps, shifts, rows_hbm, cols_hbm, out,
    image, weights, rows_table, cols_table, load_sem,
    raw, xt, edges, halo, big, table, xf, sh0, sh1, sh2, ybuf, stage,
    tile_send, tile_recv, edge_send, edge_recv, twin_send, twin_recv, out_send, out_recv,
):
    me = lax.axis_index("sub")
    place = lax.axis_index("rng")
    width = image_hbm.shape[3]
    half_size = n // 2
    block = 2 * width // n
    tiles = block // LANES
    rows = LANES + 2 * HALO
    bits = n.bit_length() - 1

    twin = place % CORES
    first = place - twin
    mine = me // half_size
    spot = me % half_size
    at_left = jnp.logical_and(place == 0, spot == 0)
    at_right = jnp.logical_and(place == rngs - 1, spot == half_size - 1)

    def tile_of(core, j):
        return j + core * (tiles - 1 - 2 * j)

    def lanes(start):
        return pl.ds(pl.multiple_of(start, LANES), LANES)

    def tile_copy(m, core, j):
        return pltpu.make_async_remote_copy(
            src_ref=image.at[:, m, :, lanes(core * block + tile_of(core, j) * LANES)],
            dst_ref=raw.at[me, j],
            send_sem=tile_send.at[m, core, j],
            recv_sem=tile_recv.at[me, j],
            device_id={"sub": m * half_size + twin, "rng": first + core},
            device_id_type=MESH,
        )

    def tile_arrival(src, j):
        return pltpu.make_async_remote_copy(
            src_ref=raw.at[src, j],
            dst_ref=raw.at[src, j],
            send_sem=tile_send.at[0, 0, 0],
            recv_sem=tile_recv.at[src, j],
            device_id={"sub": src, "rng": first + spot},
            device_id_type=MESH,
        )

    def edge_home(side, m):
        return m * half_size + 1 - twin, first + 2 * twin - side

    def edge_copy(side, m, src):
        z, r = edge_home(side, m)
        return pltpu.make_async_remote_copy(
            src_ref=edges.at[side, m],
            dst_ref=halo.at[src],
            send_sem=edge_send.at[side, m],
            recv_sem=edge_recv.at[src],
            device_id={"sub": z, "rng": r},
            device_id_type=MESH,
        )

    def twin_copy():
        return pltpu.make_async_remote_copy(
            src_ref=xt.at[:, :, pl.ds(pl.multiple_of(block - twin * (block - HALO), HALO), HALO), :],
            dst_ref=xt.at[:, :, pl.ds(pl.multiple_of(twin * (block + HALO), HALO), HALO), :],
            send_sem=twin_send,
            recv_sem=twin_recv,
            device_id={"rng": place + 1 - 2 * twin},
            device_id_type=MESH,
        )

    def out_copy(j, z):
        return pltpu.make_async_remote_copy(
            src_ref=stage.at[j, z],
            dst_ref=out.at[:, mine, :, lanes(twin * block + tile_of(twin, j) * LANES)],
            send_sem=out_send.at[j, z],
            recv_sem=out_recv.at[mine, twin, j],
            device_id={"sub": z, "rng": first + spot},
            device_id_type=MESH,
        )

    def out_arrival(h, core, j):
        return pltpu.make_async_remote_copy(
            src_ref=stage.at[j, 0],
            dst_ref=out.at[:, h, :, lanes(core * block + tile_of(core, j) * LANES)],
            send_sem=out_send.at[0, 0],
            recv_sem=out_recv.at[h, core, j],
            device_id={"sub": h * half_size + twin, "rng": first + core},
            device_id_type=MESH,
        )

    def differs(z, r):
        return jnp.logical_or(me != z, place != r)

    barrier = pltpu.get_barrier_semaphore()

    def ready(cond, z, r):
        @pl.when(cond)
        def _():
            pl.semaphore_signal(
                barrier, inc=1, device_id={"sub": z, "rng": r}, device_id_type=MESH
            )

    head_from_left = jnp.logical_and(spot == 0, jnp.logical_and(twin == 0, place > 0))
    tail_from_right = jnp.logical_and(
        spot == half_size - 1, jnp.logical_and(twin == 1, place < rngs - 1)
    )
    for z in range(n):
        for c in range(CORES):
            ready(differs(z, first + c), z, first + c)
        ready(head_from_left, z, place - 1)
        ready(tail_from_right, z, place + 1)

    others = [
        pltpu.make_async_copy(src, dst, load_sem.at[2 + k])
        for k, (src, dst) in enumerate(
            ((weights_hbm, weights), (rows_hbm, rows_table), (cols_hbm, cols_table))
        )
    ]
    order = (1 - mine, mine)
    loads = [
        pltpu.make_async_copy(image_hbm.at[:, m], image.at[:, m], load_sem.at[k])
        for k, m in enumerate(order)
    ]
    for copy in loads + others:
        copy.start()

    goes_right = jnp.logical_or(twin == 0, place < rngs - 1)
    goes_left = jnp.logical_or(twin == 1, place > 0)
    leaves = jnp.where(twin == 1, place < rngs - 1, place > 0)
    pl.semaphore_wait(barrier, CORES * n - 1 + 2 * leaves.astype(jnp.int32))
    for copy in loads:
        copy.wait()

    def send_tiles(j):
        for core in range(CORES):
            tile_copy(1 - mine, core, j).start()
        for core in range(CORES):

            @pl.when(differs(mine * half_size + twin, first + core))
            def _():
                tile_copy(mine, core, j).start()

    send_tiles(0)

    def unit(count, shift):
        i = lax.broadcasted_iota(jnp.int32, (count, LANES), 0)
        k = lax.broadcasted_iota(jnp.int32, (count, LANES), 1)
        return (i + shift == k).astype(jnp.bfloat16)

    for side, (shift, start) in enumerate(((LANES - HALO, width - LANES), (0, 0))):
        pick = unit(HALO, shift)
        for m in range(2):
            for c in range(2):
                edges[side, m, c] = lax.dot_general(
                    pick, image[c, m, :, start : start + LANES], NT, preferred_element_type=jnp.float32
                ).astype(jnp.bfloat16)
            z, r = edge_home(side, m)
            exists = (goes_right, goes_left)[side]

            @pl.when(jnp.logical_and(exists, differs(z, r)))
            def _():
                edge_copy(side, m, me).start()

            @pl.when(jnp.logical_and(exists, jnp.logical_not(differs(z, r))))
            def _():
                halo[me] = edges[side, m]

    for j in range(1, tiles):
        send_tiles(j)

    for copy in others:
        copy.wait()

    for level in range(LEVELS):
        for half in range(2):
            for side in range(2):
                real = weights[level, side, half, 0]
                imag = weights[level, side, half, 1]
                i = half * 2 * ANGLES
                j = side * 2 * ANGLES
                big[level, i : i + ANGLES, j : j + ANGLES] = real
                big[level, i : i + ANGLES, j + ANGLES : j + 2 * ANGLES] = -imag
                big[level, i + ANGLES : i + 2 * ANGLES, j : j + ANGLES] = imag
                big[level, i + ANGLES : i + 2 * ANGLES, j + ANGLES : j + 2 * ANGLES] = real
            if level < LEVELS - 1:
                for part in range(2):
                    for start in range(0, rows, PERIOD):
                        size = min(PERIOD, rows - start)
                        table[level, half, part, start : start + size, :] = rows_table[
                            level, half, part, :size, :
                        ]

    eye = unit(LANES, 0)

    def take(j):
        at = HALO + tile_of(twin, j) * LANES

        @pl.when(twin == spot)
        def _():
            raw[me, j] = image[:, mine, :, lanes(twin * block + tile_of(twin, j) * LANES)]

        for src in range(n):

            @pl.when(differs(src, first + spot))
            def _():
                tile_arrival(src, j).wait_recv()

            for c in range(2):
                xt[src, c, pl.ds(pl.multiple_of(at, HALO), LANES), :] = lax.dot_general(
                    eye, raw[src, j, c], NT, preferred_element_type=jnp.float32
                )

    take(0)

    outer = jnp.logical_or(at_left, at_right)
    halo_at = pl.ds(pl.multiple_of(twin * (block + HALO), HALO), HALO)
    rim_at = pl.ds(pl.multiple_of(twin * (block + HALO), HALO), HALO)
    for src in range(n):
        gone = jnp.logical_and(spot != twin, src == me)

        @pl.when(jnp.logical_not(jnp.logical_or(outer, gone)))
        def _():
            edge_copy(0, 0, src).wait_recv()

    @pl.when(outer)
    def _():
        xt[:, :, halo_at, :] = jnp.zeros((n, 2, HALO, ANGLES), jnp.float32)

    @pl.when(jnp.logical_not(outer))
    def _():
        xt[:, :, rim_at, :] = halo[...].astype(jnp.float32)

    def send_back(j, s):
        here = jnp.logical_and(s == me, spot == twin)

        @pl.when(jnp.logical_not(here))
        def _():
            out_copy(j, s).start()

        @pl.when(here)
        def _():
            out[:, mine, :, lanes(twin * block + tile_of(twin, j) * LANES)] = stage[j, s]

    def per_tile(j, carry):
        @pl.when(j < tiles - 1)
        def _():
            take(j + 1)

        @pl.when(j == tiles - 2)
        def _():
            twin_copy().start()

        @pl.when(j == tiles - 1)
        def _():
            twin_copy().wait()

        start = pl.multiple_of(tile_of(twin, j) * LANES, LANES)

        for level in range(LEVELS):
            mask = 2 ** (level % bits)
            base = RIM * level
            count = rows - 2 * base
            kept = count - 2 * RIM
            wide = kept + RIM

            def per_pair(pair, inner, level=level, mask=mask, base=base, count=count, kept=kept, wide=wide):
                low = pair // mask * (2 * mask) + pair % mask
                members = (low, low + mask)
                for side in range(2):
                    k = shifts[level, side][None, :] + RIM
                    on8, on4, on2, on1 = [(k // p) % 2 == 1 for p in (8, 4, 2, 1)]
                    for c in range(2):
                        s = members[side]
                        held = xf.at[s, c] if level else xt.at[s, c, pl.ds(start, rows + 8)]
                        u = None
                        for t in range(TAPS):
                            term = taps[level, t] * held[pl.ds(base + t, count), :]
                            u = term if u is None else u + term
                        v = jnp.where(on8, u[RIM:], u[:wide])
                        sh0[:wide] = v
                        v = jnp.where(on4, sh0[pl.ds(4, wide), :], v)
                        sh1[:wide] = v
                        v = jnp.where(on2, sh1[pl.ds(2, wide), :], v)
                        sh2[:wide] = v
                        v = jnp.where(on1, sh2[pl.ds(1, kept), :], v[:kept])
                        i = (side * 2 + c) * ANGLES
                        ybuf[:kept, i : i + ANGLES] = v.astype(jnp.bfloat16)
                y = ybuf[:kept, :]
                if level < LEVELS - 1:
                    z = lax.dot_general(y, big[level], NT, preferred_element_type=jnp.float32)
                    for half in range(2):
                        s = members[half]
                        i = half * 2 * ANGLES
                        re, im = z[:, i : i + ANGLES], z[:, i + ANGLES : i + 2 * ANGLES]
                        span_rows = pl.ds(base + RIM, kept)
                        cosine = table[level, half, 0, span_rows, :]
                        sinus = table[level, half, 1, span_rows, :]
                        xf[s, 0, span_rows, :] = re * cosine - im * sinus
                        xf[s, 1, span_rows, :] = re * sinus + im * cosine
                else:
                    z = lax.dot_general(big[level], y, NT, preferred_element_type=jnp.float32)
                    for half in range(2):
                        s = members[half]
                        i = half * 2 * ANGLES
                        cosine, sinus = cols_table[half, 0], cols_table[half, 1]
                        re, im = z[i : i + ANGLES, :], z[i + ANGLES : i + 2 * ANGLES, :]
                        stage[j, s, 0] = (re * cosine - im * sinus).astype(jnp.bfloat16)
                        stage[j, s, 1] = (re * sinus + im * cosine).astype(jnp.bfloat16)
                    send_back(j, low + mask * (1 - mine))
                    send_back(j, low + mask * mine)

                return inner

            lax.fori_loop(0, n // 2, per_pair, 0)
            if level < LEVELS - 1:

                @pl.when(jnp.logical_and(at_left, j == 0))
                def _():
                    xf[:, :, :HALO, :] = jnp.zeros((n, 2, HALO, ANGLES), jnp.float32)

                @pl.when(jnp.logical_and(at_right, j == 0))
                def _():
                    xf[:, :, rows - HALO : rows, :] = jnp.zeros((n, 2, HALO, ANGLES), jnp.float32)

        return carry

    lax.fori_loop(0, tiles, per_tile, 0)

    for j in range(tiles):
        for core in range(CORES):
            tile_copy(1 - mine, core, j).wait_send()

            @pl.when(differs(mine * half_size + twin, first + core))
            def _():
                tile_copy(mine, core, j).wait_send()

    for side in range(2):
        for m in range(2):
            z, r = edge_home(side, m)

            @pl.when(jnp.logical_and((goes_right, goes_left)[side], differs(z, r)))
            def _():
                edge_copy(side, m, me).wait_send()

    for j in range(tiles):
        for z in range(n):

            @pl.when(differs(z, first + spot))
            def _():
                out_copy(j, z).wait_send()

        for h in range(2):
            for core in range(CORES):

                @pl.when(differs(h * half_size + twin, first + core))
                def _():
                    out_arrival(h, core, j).wait_recv()


def in_one_kernel(n, rngs, image, interp_weights, range_taps, range_shifts):
    width = image.shape[3]
    block = 2 * width // n
    tiles = block // LANES
    rows = LANES + 2 * HALO
    rows_table, cols_table = phase_tables()
    vmem = pl.BlockSpec(memory_space=pltpu.VMEM)
    hbm = pl.BlockSpec(memory_space=pl.ANY)
    dma = pltpu.SemaphoreType.DMA
    f32, bf16 = jnp.float32, jnp.bfloat16
    return pl.pallas_call(
        functools.partial(merge_kernel, n, rngs),
        out_shape=pltpu.VMEM(image.shape, bf16),
        in_specs=[hbm, hbm, pl.BlockSpec(memory_space=pltpu.SMEM), vmem, hbm, hbm],
        out_specs=vmem,
        scratch_shapes=[
            pltpu.VMEM(image.shape, bf16),
            pltpu.VMEM(interp_weights.shape, bf16),
            pltpu.VMEM(rows_table.shape, f32),
            pltpu.VMEM(cols_table.shape, f32),
            dma((5,)),
            pltpu.VMEM((n, tiles, 2, ANGLES, LANES), bf16),
            pltpu.VMEM((n, 2, block + 2 * HALO + 8, ANGLES), f32),
            pltpu.VMEM((2, 2, 2, HALO, ANGLES), bf16),
            pltpu.VMEM((n, 2, HALO, ANGLES), bf16),
            pltpu.VMEM((LEVELS, 4 * ANGLES, 4 * ANGLES), bf16),
            pltpu.VMEM((LEVELS - 1, 2, 2, rows, ANGLES), f32),
            pltpu.VMEM((n, 2, rows + 8, ANGLES), f32),
            pltpu.VMEM((rows + 8, ANGLES), f32),
            pltpu.VMEM((rows + 8, ANGLES), f32),
            pltpu.VMEM((rows + 8, ANGLES), f32),
            pltpu.VMEM((rows, 4 * ANGLES), bf16),
            pltpu.VMEM((tiles, n, 2, ANGLES, LANES), bf16),
            dma((2, CORES, tiles)),
            dma((n, tiles)),
            dma((2, 2)),
            dma((n,)),
            dma(()),
            dma(()),
            dma((tiles, n)),
            dma((2, CORES, tiles)),
        ],
        compiler_params=pltpu.CompilerParams(has_side_effects=True, collective_id=0),
    )(image, interp_weights, range_taps, range_shifts, rows_table, cols_table)


def fits_kernel(mesh, image_shape):
    n = mesh.shape["sub"]
    paired = mesh.shape["rng"] % CORES == 0
    tiled = image_shape[3] % (CORES * LANES) == 0 and image_shape[3] > CORES * LANES
    return paired and n == 2 * CORES and image_shape[1] == 2 and tiled and ANGLES == LANES


def per_device(mesh, image, *rest):
    if fits_kernel(mesh, image.shape):
        return in_one_kernel(mesh.shape["sub"], mesh.shape["rng"], image, *rest)
    return on_device(image, *rest)


def solution(mesh):
    return jax.shard_map(
        functools.partial(per_device, mesh),
        mesh=mesh,
        in_specs=(P(None, ("img", "sub"), None, "rng"), P(), P(), P()),
        out_specs=P(None, ("img", "sub"), None, "rng"),
        check_vma=False,
    )
```

time: 57.5 us -> 54.3 us (0.944)
  the two profiles are of different devices: /device:TPU:15 before, /device:TPU:0 now
where the time goes in v2:
time: 54.3 us; the launch traced here: 54.1 us
  Pallas kernels  53.1 us (98%)
  local copies, waits for them, and re-layouts  0.97 us (2%)
    pallas_call x1, Pallas kernels, in_one_kernel(): pl.pallas_call(functools.partial(merge_kernel, n, rngs), out_shape=pltpu....  53.1 us

profile of v2, /device:TPU:0, one launch (start us, length us, event | category | flops | bytes accessed | tf_op | source)
XLA Modules:
  0.0 54.1 jit_solution(1157505441674978896)
XLA Ops:
  0.0 53.1 %shard_map.64 = bf16[2,2,128,1024]{3,2,1,0:T(8,128)(2,1)S(1)} custom-call(bf16[2,2,128,1024]{3,2,1,0:T(8,128)(2,1)} %image_hbm.1, bf16[4,2,2,2,128,128]{5,4,3,2,1,0:T(8,128)(2,1)} %weights_hbm.1, f32[4,4]{1,0:T(4,128)} %taps.1, s32[4,2,128]{2,1,0:T(2,128)} %shifts.1, f32[3,2,2,64,128]{4,3,2,1,0:T(8,128)} %constant.4.clone.rows_hbm, ...), custom_call_target="tpu_custom_call" | custom-call | tf_op jit(solution)/shard_map/pallas_call | solution.py:533
  53.1 1.0 %copy.8 = bf16[2,2,128,1024]{3,2,1,0:T(8,128)(2,1)} copy(bf16[2,2,128,1024]{3,2,1,0:T(8,128)(2,1)S(1)} %shard_map.64) | data formatting | bytes 2097152

commit v3 on v2

--- a/solution.py
+++ b/solution.py
@@ -160,10 +160,11 @@
 
 
 def merge_kernel(
-    n, rngs, image_hbm, weights_hbm, taps, shifts, rows_hbm, cols_hbm, out,
-    image, weights, rows_table, cols_table, load_sem,
+    n, rngs, image_hbm, weights_hbm, taps_hbm, shifts_hbm, rows_hbm, cols_hbm, out,
+    image, weights, taps, shifts, rows_table, cols_table, load_sem,
     raw, xt, edges, halo, big, table, xf, sh0, sh1, sh2, ybuf, stage,
     tile_send, tile_recv, edge_send, edge_recv, twin_send, twin_recv, out_send, out_recv,
+    meet_send, meet_recv, seen, met,
 ):
     me = lax.axis_index("sub")
     place = lax.axis_index("rng")
@@ -178,46 +179,68 @@
     first = place - twin
     mine = me // half_size
     spot = me % half_size
-    at_left = jnp.logical_and(place == 0, spot == 0)
-    at_right = jnp.logical_and(place == rngs - 1, spot == half_size - 1)
+    flip = place // CORES % 2
+    home = twin + flip * (1 - 2 * twin)
+    origin = spot + flip * (1 - 2 * spot)
+    inner = twin != origin
+    at_left = jnp.logical_and(place == 0, origin == 0)
+    at_right = jnp.logical_and(place == rngs - 1, origin == CORES - 1)
+    meets = jnp.logical_not(jnp.logical_or(inner, jnp.logical_or(at_left, at_right)))
+    meets_right = jnp.logical_and(meets, twin == 1)
+    meets_left = jnp.logical_and(meets, twin == 0)
+    across = 1 - 2 * twin
 
     def tile_of(core, j):
         return j + core * (tiles - 1 - 2 * j)
 
-    def lanes(start):
-        return pl.ds(pl.multiple_of(start, LANES), LANES)
-
-    def tile_copy(m, core, j):
+    def lanes(start, count=1):
+        return pl.ds(pl.multiple_of(start, LANES), count * LANES)
+
+    def columns(core, j, count=1):
+        return tile_of(core, j) * LANES - core * (count - 1) * LANES
+
+    def part_copy(m, core, part):
+        j, count = (0, 2) if part == 0 else (part + 1, 1)
+        start = columns(core, j, count)
         return pltpu.make_async_remote_copy(
-            src_ref=image.at[:, m, :, lanes(core * block + tile_of(core, j) * LANES)],
-            dst_ref=raw.at[me, j],
-            send_sem=tile_send.at[m, core, j],
-            recv_sem=tile_recv.at[me, j],
-            device_id={"sub": m * half_size + twin, "rng": first + core},
+            src_ref=image.at[:, m, :, lanes(core * block + start, count)],
+            dst_ref=raw.at[me, :, :, lanes(start, count)],
+            send_sem=tile_send.at[m, core, part],
+            recv_sem=tile_recv.at[me, part],
+            device_id={"sub": m * half_size + home, "rng": first + core},
             device_id_type=MESH,
         )
 
-    def tile_arrival(src, j):
+    def part_arrival(src, part, count):
+        here = raw.at[src, :, :, lanes(0, count)]
         return pltpu.make_async_remote_copy(
-            src_ref=raw.at[src, j],
-            dst_ref=raw.at[src, j],
+            src_ref=here,
+            dst_ref=here,
             send_sem=tile_send.at[0, 0, 0],
-            recv_sem=tile_recv.at[src, j],
-            device_id={"sub": src, "rng": first + spot},
+            recv_sem=tile_recv.at[src, part],
+            device_id={"sub": src, "rng": first + origin},
             device_id_type=MESH,
         )
 
-    def edge_home(side, m):
-        return m * half_size + 1 - twin, first + 2 * twin - side
-
-    def edge_copy(side, m, src):
-        z, r = edge_home(side, m)
+    def edge_copy(m, src):
         return pltpu.make_async_remote_copy(
-            src_ref=edges.at[side, m],
+            src_ref=edges.at[m],
             dst_ref=halo.at[src],
-            send_sem=edge_send.at[side, m],
+            send_sem=edge_send.at[m],
             recv_sem=edge_recv.at[src],
-            device_id={"sub": z, "rng": r},
+            device_id={"sub": m * half_size + 1 - home},
+            device_id_type=MESH,
+        )
+
+    def meet_copy():
+        return pltpu.make_async_remote_copy(
+            src_ref=xt.at[:, :, pl.ds(pl.multiple_of(HALO + twin * (block - HALO), HALO), HALO), :],
+            dst_ref=xt.at[
+                :, :, pl.ds(pl.multiple_of((1 - twin) * (block + HALO), HALO), HALO), :
+            ],
+            send_sem=meet_send,
+            recv_sem=meet_recv,
+            device_id={"rng": place - across},
             device_id_type=MESH,
         )
 
@@ -231,105 +254,146 @@
             device_id_type=MESH,
         )
 
-    def out_copy(j, z):
+    def out_copy(j, count, z):
+        start = columns(twin, j, count)
         return pltpu.make_async_remote_copy(
-            src_ref=stage.at[j, z],
-            dst_ref=out.at[:, mine, :, lanes(twin * block + tile_of(twin, j) * LANES)],
+            src_ref=stage.at[z, :, :, lanes(start, count)],
+            dst_ref=out.at[:, mine, :, lanes(twin * block + start, count)],
             send_sem=out_send.at[j, z],
             recv_sem=out_recv.at[mine, twin, j],
-            device_id={"sub": z, "rng": first + spot},
+            device_id={"sub": z, "rng": first + origin},
             device_id_type=MESH,
         )
 
-    def out_arrival(h, core, j):
+    def out_arrival(h, core, j, count):
+        here = out.at[:, h, :, lanes(core * block + columns(core, j, count), count)]
         return pltpu.make_async_remote_copy(
-            src_ref=stage.at[j, 0],
-            dst_ref=out.at[:, h, :, lanes(core * block + tile_of(core, j) * LANES)],
+            src_ref=here,
+            dst_ref=here,
             send_sem=out_send.at[0, 0],
             recv_sem=out_recv.at[h, core, j],
-            device_id={"sub": h * half_size + twin, "rng": first + core},
+            device_id={"sub": h * half_size + home, "rng": first + core},
             device_id_type=MESH,
         )
 
     def differs(z, r):
         return jnp.logical_or(me != z, place != r)
 
+    def signal(sem, cond, z, r):
+        @pl.when(cond)
+        def _():
+            pl.semaphore_signal(sem, inc=1, device_id={"sub": z, "rng": r}, device_id_type=MESH)
+
+    def await_signal(sem, cond, count=1):
+        @pl.when(cond)
+        def _():
+            pl.semaphore_wait(sem, count)
+
     barrier = pltpu.get_barrier_semaphore()
-
-    def ready(cond, z, r):
-        @pl.when(cond)
-        def _():
-            pl.semaphore_signal(
-                barrier, inc=1, device_id={"sub": z, "rng": r}, device_id_type=MESH
+    for step in range(1, n):
+        for c in range(CORES):
+            signal(barrier, me + step < n, me + step, first + c)
+    pl.semaphore_signal(
+        barrier, inc=1, device_id={"rng": place + across}, device_id_type=MESH
+    )
+    signal(barrier, meets_right, me, place + 1)
+
+    def load(k, m, start, size):
+        cols = pl.ds(start, size)
+        return pltpu.make_async_copy(image_hbm.at[:, m, :, cols], image.at[:, m, :, cols], load_sem.at[k])
+
+    loads = [
+        load(0, 1 - mine, 0, 2 * LANES),
+        load(1, 1 - mine, width - 2 * LANES, 2 * LANES),
+        load(2, mine, 0, width),
+    ]
+    if width > 4 * LANES:
+        loads.append(load(3, 1 - mine, 2 * LANES, width - 4 * LANES))
+    others = [
+        pltpu.make_async_copy(src, dst, load_sem.at[4 + k])
+        for k, (src, dst) in enumerate(
+            (
+                (weights_hbm, weights),
+                (rows_hbm, rows_table),
+                (cols_hbm, cols_table),
+                (taps_hbm, taps),
+                (shifts_hbm, shifts),
             )
-
-    head_from_left = jnp.logical_and(spot == 0, jnp.logical_and(twin == 0, place > 0))
-    tail_from_right = jnp.logical_and(
-        spot == half_size - 1, jnp.logical_and(twin == 1, place < rngs - 1)
-    )
-    for z in range(n):
-        for c in range(CORES):
-            ready(differs(z, first + c), z, first + c)
-        ready(head_from_left, z, place - 1)
-        ready(tail_from_right, z, place + 1)
-
-    others = [
-        pltpu.make_async_copy(src, dst, load_sem.at[2 + k])
-        for k, (src, dst) in enumerate(
-            ((weights_hbm, weights), (rows_hbm, rows_table), (cols_hbm, cols_table))
-        )
-    ]
-    order = (1 - mine, mine)
-    loads = [
-        pltpu.make_async_copy(image_hbm.at[:, m], image.at[:, m], load_sem.at[k])
-        for k, m in enumerate(order)
+        )
     ]
     for copy in loads + others:
         copy.start()
 
-    goes_right = jnp.logical_or(twin == 0, place < rngs - 1)
-    goes_left = jnp.logical_or(twin == 1, place > 0)
-    leaves = jnp.where(twin == 1, place < rngs - 1, place > 0)
-    pl.semaphore_wait(barrier, CORES * n - 1 + 2 * leaves.astype(jnp.int32))
-    for copy in loads:
+    def send_across(part):
+        for core in range(CORES):
+            part_copy(1 - mine, core, part).start()
+
+    def send_along(part):
+        for core in range(CORES):
+
+            @pl.when(differs(mine * half_size + home, first + core))
+            def _():
+                part_copy(mine, core, part).start()
+
+    pl.semaphore_wait(barrier, 1 + CORES * me + meets_left.astype(jnp.int32))
+    for step in range(1, n):
+        for c in range(CORES):
+            signal(seen.at[step], me - step >= 0, me - step, first + c)
+    signal(met, meets_left, me, place - 1)
+    loads[0].wait()
+    loads[1].wait()
+
+    @pl.when(mine == 1)
+    def _():
+        send_across(0)
+
+    loads[2].wait()
+
+    @pl.when(home <= spot)
+    def _():
+        send_along(0)
+
+    for copy in loads[3:]:
         copy.wait()
-
-    def send_tiles(j):
-        for core in range(CORES):
-            tile_copy(1 - mine, core, j).start()
-        for core in range(CORES):
-
-            @pl.when(differs(mine * half_size + twin, first + core))
+    for step in range(1, n):
+        await_signal(seen.at[step], me + step < n, CORES)
+
+        @pl.when(jnp.logical_and(mine == 0, half_size + home - me == step))
+        def _():
+            send_across(0)
+
+        if step == 1:
+
+            @pl.when(home > spot)
             def _():
-                tile_copy(mine, core, j).start()
-
-    send_tiles(0)
+                send_along(0)
 
     def unit(count, shift):
         i = lax.broadcasted_iota(jnp.int32, (count, LANES), 0)
         k = lax.broadcasted_iota(jnp.int32, (count, LANES), 1)
         return (i + shift == k).astype(jnp.bfloat16)
 
-    for side, (shift, start) in enumerate(((LANES - HALO, width - LANES), (0, 0))):
-        pick = unit(HALO, shift)
-        for m in range(2):
-            for c in range(2):
-                edges[side, m, c] = lax.dot_general(
-                    pick, image[c, m, :, start : start + LANES], NT, preferred_element_type=jnp.float32
-                ).astype(jnp.bfloat16)
-            z, r = edge_home(side, m)
-            exists = (goes_right, goes_left)[side]
-
-            @pl.when(jnp.logical_and(exists, differs(z, r)))
-            def _():
-                edge_copy(side, m, me).start()
-
-            @pl.when(jnp.logical_and(exists, jnp.logical_not(differs(z, r))))
-            def _():
-                halo[me] = edges[side, m]
-
-    for j in range(1, tiles):
-        send_tiles(j)
+    pick = unit(HALO, (1 - twin) * (LANES - HALO))
+    for m in range(2):
+        for c in range(2):
+            edges[m, c] = lax.dot_general(
+                pick,
+                image[c, m, :, lanes((1 - twin) * (width - LANES))],
+                NT,
+                preferred_element_type=jnp.float32,
+            ).astype(jnp.bfloat16)
+
+        @pl.when(m * half_size + 1 - home != me)
+        def _():
+            edge_copy(m, me).start()
+
+        @pl.when(m * half_size + 1 - home == me)
+        def _():
+            halo[me] = edges[m]
+
+    for part in range(1, tiles - 1):
+        send_across(part)
+        send_along(part)
 
     for copy in others:
         copy.wait()
@@ -355,56 +419,71 @@
 
     eye = unit(LANES, 0)
 
+    @pl.when(twin == origin)
+    def _():
+        raw[me] = image[:, mine, :, lanes(twin * block, tiles)]
+
+    def await_part(part, count):
+        for src in range(n):
+
+            @pl.when(differs(src, first + origin))
+            def _():
+                part_arrival(src, part, count).wait_recv()
+
     def take(j):
-        at = HALO + tile_of(twin, j) * LANES
-
-        @pl.when(twin == spot)
-        def _():
-            raw[me, j] = image[:, mine, :, lanes(twin * block + tile_of(twin, j) * LANES)]
-
+        start = tile_of(twin, j) * LANES
         for src in range(n):
-
-            @pl.when(differs(src, first + spot))
+            for c in range(2):
+                xt[src, c, pl.ds(pl.multiple_of(HALO + start, HALO), LANES), :] = lax.dot_general(
+                    eye, raw[src, c, :, lanes(start)], NT, preferred_element_type=jnp.float32
+                )
+
+    await_part(0, 2)
+    take(0)
+
+    await_signal(met, meets_right)
+    halo_at = pl.ds(pl.multiple_of(twin * (block + HALO), HALO), HALO)
+
+    @pl.when(meets)
+    def _():
+        meet_copy().start()
+        meet_copy().wait()
+
+    @pl.when(inner)
+    def _():
+        for src in range(n):
+
+            @pl.when(src != me)
             def _():
-                tile_arrival(src, j).wait_recv()
-
-            for c in range(2):
-                xt[src, c, pl.ds(pl.multiple_of(at, HALO), LANES), :] = lax.dot_general(
-                    eye, raw[src, j, c], NT, preferred_element_type=jnp.float32
-                )
-
-    take(0)
-
-    outer = jnp.logical_or(at_left, at_right)
-    halo_at = pl.ds(pl.multiple_of(twin * (block + HALO), HALO), HALO)
-    rim_at = pl.ds(pl.multiple_of(twin * (block + HALO), HALO), HALO)
-    for src in range(n):
-        gone = jnp.logical_and(spot != twin, src == me)
-
-        @pl.when(jnp.logical_not(jnp.logical_or(outer, gone)))
-        def _():
-            edge_copy(0, 0, src).wait_recv()
-
-    @pl.when(outer)
+                edge_copy(0, src).wait_recv()
+
+        xt[:, :, halo_at, :] = halo[...].astype(jnp.float32)
+
+    @pl.when(jnp.logical_or(at_left, at_right))
     def _():
         xt[:, :, halo_at, :] = jnp.zeros((n, 2, HALO, ANGLES), jnp.float32)
 
-    @pl.when(jnp.logical_not(outer))
-    def _():
-        xt[:, :, rim_at, :] = halo[...].astype(jnp.float32)
-
     def send_back(j, s):
-        here = jnp.logical_and(s == me, spot == twin)
-
-        @pl.when(jnp.logical_not(here))
-        def _():
-            out_copy(j, s).start()
+        here = jnp.logical_and(s == me, origin == twin)
+
+        @pl.when(jnp.logical_and(jnp.logical_not(here), j < tiles - 2))
+        def _():
+            out_copy(j, 1, s).start()
+
+        @pl.when(jnp.logical_and(jnp.logical_not(here), j == tiles - 1))
+        def _():
+            out_copy(tiles - 2, 2, s).start()
 
         @pl.when(here)
         def _():
-            out[:, mine, :, lanes(twin * block + tile_of(twin, j) * LANES)] = stage[j, s]
+            cols = tile_of(twin, j) * LANES
+            out[:, mine, :, lanes(twin * block + cols)] = stage[s, :, :, lanes(cols)]
 
     def per_tile(j, carry):
+        @pl.when(jnp.logical_and(j > 0, j < tiles - 1))
+        def _():
+            await_part(j, 1)
+
         @pl.when(j < tiles - 1)
         def _():
             take(j + 1)
@@ -434,21 +513,22 @@
                     on8, on4, on2, on1 = [(k // p) % 2 == 1 for p in (8, 4, 2, 1)]
                     for c in range(2):
                         s = members[side]
+                        b = side * 2 + c
                         held = xf.at[s, c] if level else xt.at[s, c, pl.ds(start, rows + 8)]
                         u = None
                         for t in range(TAPS):
                             term = taps[level, t] * held[pl.ds(base + t, count), :]
                             u = term if u is None else u + term
                         v = jnp.where(on8, u[RIM:], u[:wide])
-                        sh0[:wide] = v
-                        v = jnp.where(on4, sh0[pl.ds(4, wide), :], v)
-                        sh1[:wide] = v
-                        v = jnp.where(on2, sh1[pl.ds(2, wide), :], v)
-                        sh2[:wide] = v
-                        v = jnp.where(on1, sh2[pl.ds(1, kept), :], v[:kept])
+                        sh0[b, :wide] = v
+                        v = jnp.where(on4, sh0[b, pl.ds(4, wide), :], v)
+                        sh1[b, :wide] = v
+                        v = jnp.where(on2, sh1[b, pl.ds(2, wide), :], v)
+                        sh2[b, :wide] = v
+                        v = jnp.where(on1, sh2[b, pl.ds(1, kept), :], v[:kept])
                         i = (side * 2 + c) * ANGLES
-                        ybuf[:kept, i : i + ANGLES] = v.astype(jnp.bfloat16)
-                y = ybuf[:kept, :]
+                        ybuf[pair, :kept, i : i + ANGLES] = v.astype(jnp.bfloat16)
+                y = ybuf[pair, :kept, :]
                 if level < LEVELS - 1:
                     z = lax.dot_general(y, big[level], NT, preferred_element_type=jnp.float32)
                     for half in range(2):
@@ -467,14 +547,15 @@
                         i = half * 2 * ANGLES
                         cosine, sinus = cols_table[half, 0], cols_table[half, 1]
                         re, im = z[i : i + ANGLES, :], z[i + ANGLES : i + 2 * ANGLES, :]
-                        stage[j, s, 0] = (re * cosine - im * sinus).astype(jnp.bfloat16)
-                        stage[j, s, 1] = (re * sinus + im * cosine).astype(jnp.bfloat16)
+                        stage[s, 0, :, lanes(start)] = (re * cosine - im * sinus).astype(jnp.bfloat16)
+                        stage[s, 1, :, lanes(start)] = (re * sinus + im * cosine).astype(jnp.bfloat16)
                     send_back(j, low + mask * (1 - mine))
                     send_back(j, low + mask * mine)
 
                 return inner
 
-            lax.fori_loop(0, n // 2, per_pair, 0)
+            for pair in range(n // 2):
+                per_pair(pair, 0)
             if level < LEVELS - 1:
 
                 @pl.when(jnp.logical_and(at_left, j == 0))
@@ -489,35 +570,34 @@
 
     lax.fori_loop(0, tiles, per_tile, 0)
 
-    for j in range(tiles):
+    for part in range(tiles - 1):
         for core in range(CORES):
-            tile_copy(1 - mine, core, j).wait_send()
-
-            @pl.when(differs(mine * half_size + twin, first + core))
+            part_copy(1 - mine, core, part).wait_send()
+
+            @pl.when(differs(mine * half_size + home, first + core))
             def _():
-                tile_copy(mine, core, j).wait_send()
-
-    for side in range(2):
-        for m in range(2):
-            z, r = edge_home(side, m)
-
-            @pl.when(jnp.logical_and((goes_right, goes_left)[side], differs(z, r)))
+                part_copy(mine, core, part).wait_send()
+
+    for m in range(2):
+
+        @pl.when(m * half_size + 1 - home != me)
+        def _():
+            edge_copy(m, me).wait_send()
+
+    for j in range(tiles - 1):
+        count = 1 + (j == tiles - 2)
+        for z in range(n):
+
+            @pl.when(differs(z, first + origin))
             def _():
-                edge_copy(side, m, me).wait_send()
-
-    for j in range(tiles):
-        for z in range(n):
-
-            @pl.when(differs(z, first + spot))
-            def _():
-                out_copy(j, z).wait_send()
+                out_copy(j, count, z).wait_send()
 
         for h in range(2):
             for core in range(CORES):
 
-                @pl.when(differs(h * half_size + twin, first + core))
+                @pl.when(differs(h * half_size + home, first + core))
                 def _():
-                    out_arrival(h, core, j).wait_recv()
+                    out_arrival(h, core, j, count).wait_recv()
 
 
 def in_one_kernel(n, rngs, image, interp_weights, range_taps, range_shifts):
@@ -533,34 +613,40 @@
     return pl.pallas_call(
         functools.partial(merge_kernel, n, rngs),
         out_shape=pltpu.VMEM(image.shape, bf16),
-        in_specs=[hbm, hbm, pl.BlockSpec(memory_space=pltpu.SMEM), vmem, hbm, hbm],
+        in_specs=[hbm] * 6,
         out_specs=vmem,
         scratch_shapes=[
             pltpu.VMEM(image.shape, bf16),
             pltpu.VMEM(interp_weights.shape, bf16),
+            pltpu.SMEM(range_taps.shape, f32),
+            pltpu.VMEM(range_shifts.shape, jnp.int32),
             pltpu.VMEM(rows_table.shape, f32),
             pltpu.VMEM(cols_table.shape, f32),
-            dma((5,)),
-            pltpu.VMEM((n, tiles, 2, ANGLES, LANES), bf16),
+            dma((9,)),
+            pltpu.VMEM((n, 2, ANGLES, block), bf16),
             pltpu.VMEM((n, 2, block + 2 * HALO + 8, ANGLES), f32),
-            pltpu.VMEM((2, 2, 2, HALO, ANGLES), bf16),
+            pltpu.VMEM((2, 2, HALO, ANGLES), bf16),
             pltpu.VMEM((n, 2, HALO, ANGLES), bf16),
             pltpu.VMEM((LEVELS, 4 * ANGLES, 4 * ANGLES), bf16),
             pltpu.VMEM((LEVELS - 1, 2, 2, rows, ANGLES), f32),
             pltpu.VMEM((n, 2, rows + 8, ANGLES), f32),
-            pltpu.VMEM((rows + 8, ANGLES), f32),
-            pltpu.VMEM((rows + 8, ANGLES), f32),
-            pltpu.VMEM((rows + 8, ANGLES), f32),
-            pltpu.VMEM((rows, 4 * ANGLES), bf16),
-            pltpu.VMEM((tiles, n, 2, ANGLES, LANES), bf16),
-            dma((2, CORES, tiles)),
-            dma((n, tiles)),
-            dma((2, 2)),
+            pltpu.VMEM((4, rows + 8, ANGLES), f32),
+            pltpu.VMEM((4, rows + 8, ANGLES), f32),
+            pltpu.VMEM((4, rows + 8, ANGLES), f32),
+            pltpu.VMEM((n // 2, rows, 4 * ANGLES), bf16),
+            pltpu.VMEM((n, 2, ANGLES, block), bf16),
+            dma((2, CORES, tiles - 1)),
+            dma((n, tiles - 1)),
+            dma((2,)),
             dma((n,)),
             dma(()),
             dma(()),
-            dma((tiles, n)),
-            dma((2, CORES, tiles)),
+            dma((tiles - 1, n)),
+            dma((2, CORES, tiles - 1)),
+            dma(()),
+            dma(()),
+            pltpu.SemaphoreType.REGULAR((n,)),
+            pltpu.SemaphoreType.REGULAR,
         ],
         compiler_params=pltpu.CompilerParams(has_side_effects=True, collective_id=0),
     )(image, interp_weights, range_taps, range_shifts, rows_table, cols_table)

time: 54.3 us -> 52.9 us (0.974)
  the two profiles are of different devices: /device:TPU:0 before, /device:TPU:14 now
where the time goes in v3:
time: 52.9 us; the launch traced here: 52.7 us
  Pallas kernels  51.8 us (98%)
  local copies, waits for them, and re-layouts  0.97 us (2%)
    pallas_call x1, Pallas kernels, in_one_kernel(): pl.pallas_call(functools.partial(merge_kernel, n, rngs), out_shape=pltpu....  51.8 us

profile of v3, /device:TPU:14, one launch (start us, length us, event | category | flops | bytes accessed | tf_op | source)
XLA Modules:
  0.0 52.7 jit_solution(423719442401986178)
XLA Ops:
  0.0 51.8 %shard_map.64 = bf16[2,2,128,1024]{3,2,1,0:T(8,128)(2,1)S(1)} custom-call(bf16[2,2,128,1024]{3,2,1,0:T(8,128)(2,1)} %image_hbm.1, bf16[4,2,2,2,128,128]{5,4,3,2,1,0:T(8,128)(2,1)} %weights_hbm.1, f32[4,4]{1,0:T(4,128)} %taps_hbm.1, s32[4,2,128]{2,1,0:T(2,128)} %shifts_hbm.1, f32[3,2,2,64,128]{4,3,2,1,0:T(8,128)} %constant.4.clone.rows_hbm, ...), custom_call_target="tpu_custom_call" | custom-call | tf_op jit(solution)/shard_map/pallas_call | solution.py:613
  51.8 1.0 %copy.8 = bf16[2,2,128,1024]{3,2,1,0:T(8,128)(2,1)} copy(bf16[2,2,128,1024]{3,2,1,0:T(8,128)(2,1)S(1)} %shard_map.64) | data formatting | bytes 2097152

commit v4 on v3

--- a/solution.py
+++ b/solution.py
@@ -289,15 +289,6 @@
         def _():
             pl.semaphore_wait(sem, count)
 
-    barrier = pltpu.get_barrier_semaphore()
-    for step in range(1, n):
-        for c in range(CORES):
-            signal(barrier, me + step < n, me + step, first + c)
-    pl.semaphore_signal(
-        barrier, inc=1, device_id={"rng": place + across}, device_id_type=MESH
-    )
-    signal(barrier, meets_right, me, place + 1)
-
     def load(k, m, start, size):
         cols = pl.ds(start, size)
         return pltpu.make_async_copy(image_hbm.at[:, m, :, cols], image.at[:, m, :, cols], load_sem.at[k])
@@ -323,6 +314,15 @@
     ]
     for copy in loads + others:
         copy.start()
+
+    barrier = pltpu.get_barrier_semaphore()
+    for step in range(1, n):
+        for c in range(CORES):
+            signal(barrier, me + step < n, me + step, first + c)
+    pl.semaphore_signal(
+        barrier, inc=1, device_id={"rng": place + across}, device_id_type=MESH
+    )
+    signal(barrier, meets_right, me, place + 1)
 
     def send_across(part):
         for core in range(CORES):
@@ -466,11 +466,13 @@
     def send_back(j, s):
         here = jnp.logical_and(s == me, origin == twin)
 
-        @pl.when(jnp.logical_and(jnp.logical_not(here), j < tiles - 2))
+        last = s % half_size > 0
+
+        @pl.when(jnp.logical_and(jnp.logical_not(here), jnp.logical_or(j < tiles - 2, jnp.logical_not(last))))
         def _():
             out_copy(j, 1, s).start()
 
-        @pl.when(jnp.logical_and(jnp.logical_not(here), j == tiles - 1))
+        @pl.when(jnp.logical_and(jnp.logical_not(here), jnp.logical_and(j == tiles - 1, last)))
         def _():
             out_copy(tiles - 2, 2, s).start()
 
@@ -505,8 +507,8 @@
             kept = count - 2 * RIM
             wide = kept + RIM
 
-            def per_pair(pair, inner, level=level, mask=mask, base=base, count=count, kept=kept, wide=wide):
-                low = pair // mask * (2 * mask) + pair % mask
+            pairs = [(p // mask * (2 * mask) + p % mask) for p in range(n // 2)]
+            for pair, low in enumerate(pairs):
                 members = (low, low + mask)
                 for side in range(2):
                     k = shifts[level, side][None, :] + RIM
@@ -526,36 +528,40 @@
                         v = jnp.where(on2, sh1[b, pl.ds(2, wide), :], v)
                         sh2[b, :wide] = v
                         v = jnp.where(on1, sh2[b, pl.ds(1, kept), :], v[:kept])
-                        i = (side * 2 + c) * ANGLES
-                        ybuf[pair, :kept, i : i + ANGLES] = v.astype(jnp.bfloat16)
-                y = ybuf[pair, :kept, :]
-                if level < LEVELS - 1:
-                    z = lax.dot_general(y, big[level], NT, preferred_element_type=jnp.float32)
+                        i = b * ANGLES
+                        ybuf[pair * kept : (pair + 1) * kept, i : i + ANGLES] = v.astype(jnp.bfloat16)
+            y = ybuf[: n // 2 * kept, :]
+            if level < LEVELS - 1:
+                z = lax.dot_general(y, big[level], NT, preferred_element_type=jnp.float32)
+                for pair, low in enumerate(pairs):
                     for half in range(2):
-                        s = members[half]
+                        s = low + half * mask
                         i = half * 2 * ANGLES
-                        re, im = z[:, i : i + ANGLES], z[:, i + ANGLES : i + 2 * ANGLES]
+                        r = pair * kept
+                        re = z[r : r + kept, i : i + ANGLES]
+                        im = z[r : r + kept, i + ANGLES : i + 2 * ANGLES]
                         span_rows = pl.ds(base + RIM, kept)
                         cosine = table[level, half, 0, span_rows, :]
                         sinus = table[level, half, 1, span_rows, :]
                         xf[s, 0, span_rows, :] = re * cosine - im * sinus
                         xf[s, 1, span_rows, :] = re * sinus + im * cosine
-                else:
-                    z = lax.dot_general(big[level], y, NT, preferred_element_type=jnp.float32)
+            else:
+                z = lax.dot_general(big[level], y, NT, preferred_element_type=jnp.float32)
+                for pair, low in enumerate(pairs):
                     for half in range(2):
-                        s = members[half]
+                        s = low + half * mask
                         i = half * 2 * ANGLES
                         cosine, sinus = cols_table[half, 0], cols_table[half, 1]
-                        re, im = z[i : i + ANGLES, :], z[i + ANGLES : i + 2 * ANGLES, :]
+                        r = pair * kept
+                        re = z[i : i + ANGLES, r : r + kept]
+                        im = z[i + ANGLES : i + 2 * ANGLES, r : r + kept]
                         stage[s, 0, :, lanes(start)] = (re * cosine - im * sinus).astype(jnp.bfloat16)
                         stage[s, 1, :, lanes(start)] = (re * sinus + im * cosine).astype(jnp.bfloat16)
+                for low in pairs:
                     send_back(j, low + mask * (1 - mine))
+                for low in pairs:
                     send_back(j, low + mask * mine)
 
-                return inner
-
-            for pair in range(n // 2):
-                per_pair(pair, 0)
             if level < LEVELS - 1:
 
                 @pl.when(jnp.logical_and(at_left, j == 0))
@@ -584,20 +590,41 @@
         def _():
             edge_copy(m, me).wait_send()
 
-    for j in range(tiles - 1):
-        count = 1 + (j == tiles - 2)
+    merges = spot > 0
+    for j in range(tiles):
         for z in range(n):
-
-            @pl.when(differs(z, first + origin))
-            def _():
-                out_copy(j, count, z).wait_send()
+            if j < tiles - 2 or z % half_size == 0:
+
+                @pl.when(differs(z, first + origin))
+                def _():
+                    out_copy(j, 1, z).wait_send()
+
+            elif j == tiles - 2:
+
+                @pl.when(differs(z, first + origin))
+                def _():
+                    out_copy(j, 2, z).wait_send()
 
         for h in range(2):
             for core in range(CORES):
-
-                @pl.when(differs(h * half_size + home, first + core))
-                def _():
-                    out_arrival(h, core, j, count).wait_recv()
+                arrives = differs(h * half_size + home, first + core)
+                if j < tiles - 2:
+
+                    @pl.when(arrives)
+                    def _():
+                        out_arrival(h, core, j, 1).wait_recv()
+
+                else:
+
+                    @pl.when(jnp.logical_and(arrives, jnp.logical_not(merges)))
+                    def _():
+                        out_arrival(h, core, j, 1).wait_recv()
+
+                    if j == tiles - 2:
+
+                        @pl.when(jnp.logical_and(arrives, merges))
+                        def _():
+                            out_arrival(h, core, j, 2).wait_recv()
 
 
 def in_one_kernel(n, rngs, image, interp_weights, range_taps, range_shifts):
@@ -633,7 +660,7 @@
             pltpu.VMEM((4, rows + 8, ANGLES), f32),
             pltpu.VMEM((4, rows + 8, ANGLES), f32),
             pltpu.VMEM((4, rows + 8, ANGLES), f32),
-            pltpu.VMEM((n // 2, rows, 4 * ANGLES), bf16),
+            pltpu.VMEM((n // 2 * rows, 4 * ANGLES), bf16),
             pltpu.VMEM((n, 2, ANGLES, block), bf16),
             dma((2, CORES, tiles - 1)),
             dma((n, tiles - 1)),
@@ -641,8 +668,8 @@
             dma((n,)),
             dma(()),
             dma(()),
-            dma((tiles - 1, n)),
-            dma((2, CORES, tiles - 1)),
+            dma((tiles, n)),
+            dma((2, CORES, tiles)),
             dma(()),
             dma(()),
             pltpu.SemaphoreType.REGULAR((n,)),

time: 52.9 us -> 51.7 us (0.977)
  the two profiles are of different devices: /device:TPU:14 before, /device:TPU:0 now
where the time goes in v4:
time: 51.7 us; the launch traced here: 51.6 us
  Pallas kernels  50.6 us (98%)
  local copies, waits for them, and re-layouts  0.97 us (2%)
    pallas_call x1, Pallas kernels, in_one_kernel(): pl.pallas_call(functools.partial(merge_kernel, n, rngs), out_shape=pltpu....  50.6 us

profile of v4, /device:TPU:0, one launch (start us, length us, event | category | flops | bytes accessed | tf_op | source)
XLA Modules:
  0.0 51.6 jit_solution(8619847020514305730)
XLA Ops:
  0.0 50.6 %shard_map.64 = bf16[2,2,128,1024]{3,2,1,0:T(8,128)(2,1)S(1)} custom-call(bf16[2,2,128,1024]{3,2,1,0:T(8,128)(2,1)} %image_hbm.1, bf16[4,2,2,2,128,128]{5,4,3,2,1,0:T(8,128)(2,1)} %weights_hbm.1, f32[4,4]{1,0:T(4,128)} %taps_hbm.1, s32[4,2,128]{2,1,0:T(2,128)} %shifts_hbm.1, f32[3,2,2,64,128]{4,3,2,1,0:T(8,128)} %constant.4.clone.rows_hbm, ...), custom_call_target="tpu_custom_call" | custom-call | tf_op jit(solution)/shard_map/pallas_call | solution.py:640
  50.6 1.0 %copy.8 = bf16[2,2,128,1024]{3,2,1,0:T(8,128)(2,1)} copy(bf16[2,2,128,1024]{3,2,1,0:T(8,128)(2,1)S(1)} %shard_map.64) | data formatting | bytes 2097152

commit v5 on v4

--- a/solution.py
+++ b/solution.py
@@ -159,12 +159,16 @@
     return tables[: LEVELS - 1], last
 
 
+def tile_parts(tiles):
+    return [(0, 2), *[(j, 1) for j in range(2, tiles)]]
+
+
 def merge_kernel(
     n, rngs, image_hbm, weights_hbm, taps_hbm, shifts_hbm, rows_hbm, cols_hbm, out,
     image, weights, taps, shifts, rows_table, cols_table, load_sem,
-    raw, xt, edges, halo, big, table, xf, sh0, sh1, sh2, ybuf, stage,
-    tile_send, tile_recv, edge_send, edge_recv, twin_send, twin_recv, out_send, out_recv,
-    meet_send, meet_recv, seen, met,
+    raw, xt, big, table, xf, sh0, sh1, sh2, ybuf, stage,
+    tile_send, tile_recv, twin_send, twin_recv, out_send, out_recv,
+    rim_send, rim_recv, seen, met,
 ):
     me = lax.axis_index("sub")
     place = lax.axis_index("rng")
@@ -174,6 +178,9 @@
     tiles = block // LANES
     rows = LANES + 2 * HALO
     bits = n.bit_length() - 1
+    pairs = [(j, min(2, tiles - j)) for j in range(0, tiles, 2)]
+    parts = tile_parts(tiles)
+    plans = ([(j, 1) for j in range(tiles)], [*[(j, 1) for j in range(pairs[-1][0])], pairs[-1]])
 
     twin = place % CORES
     first = place - twin
@@ -189,6 +196,8 @@
     meets_right = jnp.logical_and(meets, twin == 1)
     meets_left = jnp.logical_and(meets, twin == 0)
     across = 1 - 2 * twin
+    rim_sub = jnp.where(inner, mine * half_size + half_size - 1 - spot, me)
+    rim_rng = jnp.where(inner, place + across, place - across)
 
     def tile_of(core, j):
         return j + core * (tiles - 1 - 2 * j)
@@ -199,11 +208,11 @@
     def columns(core, j, count=1):
         return tile_of(core, j) * LANES - core * (count - 1) * LANES
 
-    def part_copy(m, core, part):
-        j, count = (0, 2) if part == 0 else (part + 1, 1)
+    def part_copy(m, core, part, source=None):
+        j, count = parts[part]
         start = columns(core, j, count)
         return pltpu.make_async_remote_copy(
-            src_ref=image.at[:, m, :, lanes(core * block + start, count)],
+            src_ref=(image if source is None else source).at[:, m, :, lanes(core * block + start, count)],
             dst_ref=raw.at[me, :, :, lanes(start, count)],
             send_sem=tile_send.at[m, core, part],
             recv_sem=tile_recv.at[me, part],
@@ -222,25 +231,15 @@
             device_id_type=MESH,
         )
 
-    def edge_copy(m, src):
-        return pltpu.make_async_remote_copy(
-            src_ref=edges.at[m],
-            dst_ref=halo.at[src],
-            send_sem=edge_send.at[m],
-            recv_sem=edge_recv.at[src],
-            device_id={"sub": m * half_size + 1 - home},
-            device_id_type=MESH,
-        )
-
-    def meet_copy():
+    def rim_copy():
         return pltpu.make_async_remote_copy(
             src_ref=xt.at[:, :, pl.ds(pl.multiple_of(HALO + twin * (block - HALO), HALO), HALO), :],
             dst_ref=xt.at[
                 :, :, pl.ds(pl.multiple_of((1 - twin) * (block + HALO), HALO), HALO), :
             ],
-            send_sem=meet_send,
-            recv_sem=meet_recv,
-            device_id={"rng": place - across},
+            send_sem=rim_send,
+            recv_sem=rim_recv,
+            device_id={"sub": rim_sub, "rng": rim_rng},
             device_id_type=MESH,
         )
 
@@ -340,12 +339,14 @@
         for c in range(CORES):
             signal(seen.at[step], me - step >= 0, me - step, first + c)
     signal(met, meets_left, me, place - 1)
+
+    @pl.when(mine == 1)
+    def _():
+        for core in range(CORES):
+            part_copy(1 - mine, core, 0, image_hbm).start()
+
     loads[0].wait()
     loads[1].wait()
-
-    @pl.when(mine == 1)
-    def _():
-        send_across(0)
 
     loads[2].wait()
 
@@ -373,25 +374,7 @@
         k = lax.broadcasted_iota(jnp.int32, (count, LANES), 1)
         return (i + shift == k).astype(jnp.bfloat16)
 
-    pick = unit(HALO, (1 - twin) * (LANES - HALO))
-    for m in range(2):
-        for c in range(2):
-            edges[m, c] = lax.dot_general(
-                pick,
-                image[c, m, :, lanes((1 - twin) * (width - LANES))],
-                NT,
-                preferred_element_type=jnp.float32,
-            ).astype(jnp.bfloat16)
-
-        @pl.when(m * half_size + 1 - home != me)
-        def _():
-            edge_copy(m, me).start()
-
-        @pl.when(m * half_size + 1 - home == me)
-        def _():
-            halo[me] = edges[m]
-
-    for part in range(1, tiles - 1):
+    for part in range(1, len(parts) - 1):
         send_across(part)
         send_along(part)
 
@@ -438,43 +421,36 @@
                     eye, raw[src, c, :, lanes(start)], NT, preferred_element_type=jnp.float32
                 )
 
-    await_part(0, 2)
+    await_part(0, parts[0][1])
     take(0)
 
     await_signal(met, meets_right)
     halo_at = pl.ds(pl.multiple_of(twin * (block + HALO), HALO), HALO)
-
-    @pl.when(meets)
+    ends = jnp.logical_or(at_left, at_right)
+
+    @pl.when(jnp.logical_not(ends))
     def _():
-        meet_copy().start()
-        meet_copy().wait()
-
-    @pl.when(inner)
+        rim_copy().start()
+
+    for part in range(max(1, len(parts) - 1), len(parts)):
+        send_across(part)
+        send_along(part)
+
+    @pl.when(jnp.logical_not(ends))
     def _():
-        for src in range(n):
-
-            @pl.when(src != me)
-            def _():
-                edge_copy(0, src).wait_recv()
-
-        xt[:, :, halo_at, :] = halo[...].astype(jnp.float32)
-
-    @pl.when(jnp.logical_or(at_left, at_right))
+        rim_copy().wait()
+
+    @pl.when(ends)
     def _():
         xt[:, :, halo_at, :] = jnp.zeros((n, 2, HALO, ANGLES), jnp.float32)
 
-    def send_back(j, s):
+    def send_back(j, s, far):
         here = jnp.logical_and(s == me, origin == twin)
-
-        last = s % half_size > 0
-
-        @pl.when(jnp.logical_and(jnp.logical_not(here), jnp.logical_or(j < tiles - 2, jnp.logical_not(last))))
-        def _():
-            out_copy(j, 1, s).start()
-
-        @pl.when(jnp.logical_and(jnp.logical_not(here), jnp.logical_and(j == tiles - 1, last)))
-        def _():
-            out_copy(tiles - 2, 2, s).start()
+        for start, count in plans[far]:
+
+            @pl.when(jnp.logical_and(jnp.logical_not(here), j == start + count - 1))
+            def _():
+                out_copy(start, count, s).start()
 
         @pl.when(here)
         def _():
@@ -482,9 +458,11 @@
             out[:, mine, :, lanes(twin * block + cols)] = stage[s, :, :, lanes(cols)]
 
     def per_tile(j, carry):
-        @pl.when(jnp.logical_and(j > 0, j < tiles - 1))
-        def _():
-            await_part(j, 1)
+        for part in range(1, len(parts)):
+
+            @pl.when(j + 1 == parts[part][0])
+            def _():
+                await_part(part, parts[part][1])
 
         @pl.when(j < tiles - 1)
         def _():
@@ -557,10 +535,9 @@
                         im = z[i + ANGLES : i + 2 * ANGLES, r : r + kept]
                         stage[s, 0, :, lanes(start)] = (re * cosine - im * sinus).astype(jnp.bfloat16)
                         stage[s, 1, :, lanes(start)] = (re * sinus + im * cosine).astype(jnp.bfloat16)
-                for low in pairs:
-                    send_back(j, low + mask * (1 - mine))
-                for low in pairs:
-                    send_back(j, low + mask * mine)
+                for group in (1 - mine, mine):
+                    for spot_to in range(half_size):
+                        send_back(j, group * half_size + spot_to, spot_to > 0)
 
             if level < LEVELS - 1:
 
@@ -576,7 +553,7 @@
 
     lax.fori_loop(0, tiles, per_tile, 0)
 
-    for part in range(tiles - 1):
+    for part in range(len(parts)):
         for core in range(CORES):
             part_copy(1 - mine, core, part).wait_send()
 
@@ -584,47 +561,22 @@
             def _():
                 part_copy(mine, core, part).wait_send()
 
-    for m in range(2):
-
-        @pl.when(m * half_size + 1 - home != me)
-        def _():
-            edge_copy(m, me).wait_send()
-
-    merges = spot > 0
-    for j in range(tiles):
-        for z in range(n):
-            if j < tiles - 2 or z % half_size == 0:
-
-                @pl.when(differs(z, first + origin))
-                def _():
-                    out_copy(j, 1, z).wait_send()
-
-            elif j == tiles - 2:
-
-                @pl.when(differs(z, first + origin))
-                def _():
-                    out_copy(j, 2, z).wait_send()
-
-        for h in range(2):
-            for core in range(CORES):
-                arrives = differs(h * half_size + home, first + core)
-                if j < tiles - 2:
-
-                    @pl.when(arrives)
+    for far, plan in enumerate(plans):
+        for start, count in plan:
+            for z in range(n):
+                if (z % half_size > 0) == far:
+
+                    @pl.when(differs(z, first + origin))
                     def _():
-                        out_arrival(h, core, j, 1).wait_recv()
-
-                else:
-
-                    @pl.when(jnp.logical_and(arrives, jnp.logical_not(merges)))
+                        out_copy(start, count, z).wait_send()
+
+            for h in range(2):
+                for core in range(CORES):
+                    arrives = differs(h * half_size + home, first + core)
+
+                    @pl.when(jnp.logical_and(arrives, (spot > 0) == far))
                     def _():
-                        out_arrival(h, core, j, 1).wait_recv()
-
-                    if j == tiles - 2:
-
-                        @pl.when(jnp.logical_and(arrives, merges))
-                        def _():
-                            out_arrival(h, core, j, 2).wait_recv()
+                        out_arrival(h, core, start, count).wait_recv()
 
 
 def in_one_kernel(n, rngs, image, interp_weights, range_taps, range_shifts):
@@ -632,6 +584,7 @@
     block = 2 * width // n
     tiles = block // LANES
     rows = LANES + 2 * HALO
+    parts = len(tile_parts(tiles))
     rows_table, cols_table = phase_tables()
     vmem = pl.BlockSpec(memory_space=pltpu.VMEM)
     hbm = pl.BlockSpec(memory_space=pl.ANY)
@@ -652,8 +605,6 @@
             dma((9,)),
             pltpu.VMEM((n, 2, ANGLES, block), bf16),
             pltpu.VMEM((n, 2, block + 2 * HALO + 8, ANGLES), f32),
-            pltpu.VMEM((2, 2, HALO, ANGLES), bf16),
-            pltpu.VMEM((n, 2, HALO, ANGLES), bf16),
             pltpu.VMEM((LEVELS, 4 * ANGLES, 4 * ANGLES), bf16),
             pltpu.VMEM((LEVELS - 1, 2, 2, rows, ANGLES), f32),
             pltpu.VMEM((n, 2, rows + 8, ANGLES), f32),
@@ -662,10 +613,8 @@
             pltpu.VMEM((4, rows + 8, ANGLES), f32),
             pltpu.VMEM((n // 2 * rows, 4 * ANGLES), bf16),
             pltpu.VMEM((n, 2, ANGLES, block), bf16),
-            dma((2, CORES, tiles - 1)),
-            dma((n, tiles - 1)),
-            dma((2,)),
-            dma((n,)),
+            dma((2, CORES, parts)),
+            dma((n, parts)),
             dma(()),
             dma(()),
             dma((tiles, n)),

time: 51.7 us -> 51.2 us (level)
  the two profiles are of different devices: /device:TPU:0 before, /device:TPU:15 now
where the time goes in v5:
time: 51.2 us; the launch traced here: 51.1 us
  Pallas kernels  50.1 us (98%)
  local copies, waits for them, and re-layouts  0.97 us (2%)
    pallas_call x1, Pallas kernels, in_one_kernel(): pl.pallas_call(functools.partial(merge_kernel, n, rngs), out_shape=pltpu....  50.1 us

profile of v5, /device:TPU:15, one launch (start us, length us, event | category | flops | bytes accessed | tf_op | source)
XLA Modules:
  0.0 51.1 jit_solution(15017828525836741966)
XLA Ops:
  0.0 50.1 %shard_map.64 = bf16[2,2,128,1024]{3,2,1,0:T(8,128)(2,1)S(1)} custom-call(bf16[2,2,128,1024]{3,2,1,0:T(8,128)(2,1)} %image_hbm.1, bf16[4,2,2,2,128,128]{5,4,3,2,1,0:T(8,128)(2,1)} %weights_hbm.1, f32[4,4]{1,0:T(4,128)} %taps_hbm.1, s32[4,2,128]{2,1,0:T(2,128)} %shifts_hbm.1, f32[3,2,2,64,128]{4,3,2,1,0:T(8,128)} %constant.4.clone.rows_hbm, ...), custom_call_target="tpu_custom_call" | custom-call | tf_op jit(solution)/shard_map/pallas_call | solution.py:593
  50.1 1.0 %copy.8 = bf16[2,2,128,1024]{3,2,1,0:T(8,128)(2,1)} copy(bf16[2,2,128,1024]{3,2,1,0:T(8,128)(2,1)S(1)} %shard_map.64) | data formatting | bytes 2097152

commit v6 on v5

--- a/solution.py
+++ b/solution.py
@@ -374,9 +374,16 @@
         k = lax.broadcasted_iota(jnp.int32, (count, LANES), 1)
         return (i + shift == k).astype(jnp.bfloat16)
 
-    for part in range(1, len(parts) - 1):
-        send_across(part)
-        send_along(part)
+    holds = me == half_size - 1
+
+    def send_middle():
+        for part in range(1, len(parts) - 1):
+            send_across(part)
+            send_along(part)
+
+    @pl.when(jnp.logical_not(holds))
+    def _():
+        send_middle()
 
     for copy in others:
         copy.wait()
@@ -421,7 +428,21 @@
                     eye, raw[src, c, :, lanes(start)], NT, preferred_element_type=jnp.float32
                 )
 
-    await_part(0, parts[0][1])
+    def await_first(srcs):
+        for src in srcs:
+
+            @pl.when(differs(src, first + origin))
+            def _():
+                part_arrival(src, 0, parts[0][1]).wait_recv()
+
+    inner_srcs = (half_size - 1, half_size)
+    await_first(inner_srcs)
+
+    @pl.when(holds)
+    def _():
+        send_middle()
+
+    await_first([src for src in range(n) if src not in inner_srcs])
     take(0)
 
     await_signal(met, meets_right)
@@ -447,8 +468,11 @@
     def send_back(j, s, far):
         here = jnp.logical_and(s == me, origin == twin)
         for start, count in plans[far]:
-
-            @pl.when(jnp.logical_and(jnp.logical_not(here), j == start + count - 1))
+            goes = jnp.logical_and(jnp.logical_not(here), j == start + count - 1)
+            if far and start + count == tiles:
+                goes = jnp.logical_and(goes, jnp.logical_or(mine == 0, s >= half_size))
+
+            @pl.when(goes)
             def _():
                 out_copy(start, count, s).start()
 
@@ -553,6 +577,12 @@
 
     lax.fori_loop(0, tiles, per_tile, 0)
 
+    @pl.when(mine == 1)
+    def _():
+        out_copy(*plans[0][-1], 0).wait_send()
+        for z in range(1, half_size):
+            out_copy(*plans[1][-1], z).start()
+
     for part in range(len(parts)):
         for core in range(CORES):
             part_copy(1 - mine, core, part).wait_send()
@@ -566,7 +596,11 @@
             for z in range(n):
                 if (z % half_size > 0) == far:
 
-                    @pl.when(differs(z, first + origin))
+                    waits = differs(z, first + origin)
+                    if z == 0 and start + count == tiles:
+                        waits = jnp.logical_and(waits, mine == 0)
+
+                    @pl.when(waits)
                     def _():
                         out_copy(start, count, z).wait_send()
 

time: 51.2 us -> 50.7 us (level)
  Pallas kernels: 50.1 us -> 49.2 us
    pallas_call x1, Pallas kernels: 50.1 us -> 49.2 us  [in_one_kernel(): pl.pallas_call(functools.partial(merge_kernel, n, rngs), out_shape=pltpu....]
where the time goes in v6:
time: 50.7 us; the launch traced here: 50.1 us
  Pallas kernels  49.2 us (97%)
  local copies, waits for them, and re-layouts  0.97 us (2%)
    pallas_call x1, Pallas kernels, in_one_kernel(): pl.pallas_call(functools.partial(merge_kernel, n, rngs), out_shape=pltpu....  49.2 us

profile of v6, /device:TPU:15, one launch (start us, length us, event | category | flops | bytes accessed | tf_op | source)
XLA Modules:
  0.0 50.1 jit_solution(8504856905170680394)
XLA Ops:
  0.0 49.2 %shard_map.64 = bf16[2,2,128,1024]{3,2,1,0:T(8,128)(2,1)S(1)} custom-call(bf16[2,2,128,1024]{3,2,1,0:T(8,128)(2,1)} %image_hbm.1, bf16[4,2,2,2,128,128]{5,4,3,2,1,0:T(8,128)(2,1)} %weights_hbm.1, f32[4,4]{1,0:T(4,128)} %taps_hbm.1, s32[4,2,128]{2,1,0:T(2,128)} %shifts_hbm.1, f32[3,2,2,64,128]{4,3,2,1,0:T(8,128)} %constant.4.clone.rows_hbm, ...), custom_call_target="tpu_custom_call" | custom-call | tf_op jit(solution)/shard_map/pallas_call | solution.py:627
  49.2 1.0 %copy.8 = bf16[2,2,128,1024]{3,2,1,0:T(8,128)(2,1)} copy(bf16[2,2,128,1024]{3,2,1,0:T(8,128)(2,1)S(1)} %shard_map.64) | data formatting | bytes 2097152

commit v7 on v6

--- a/solution.py
+++ b/solution.py
@@ -311,7 +311,7 @@
             )
         )
     ]
-    for copy in loads + others:
+    for copy in loads[:2]:
         copy.start()
 
     barrier = pltpu.get_barrier_semaphore()
@@ -345,6 +345,8 @@
         for core in range(CORES):
             part_copy(1 - mine, core, 0, image_hbm).start()
 
+    for copy in loads[2:] + others:
+        copy.start()
     loads[0].wait()
     loads[1].wait()
 
@@ -435,7 +437,7 @@
             def _():
                 part_arrival(src, 0, parts[0][1]).wait_recv()
 
-    inner_srcs = (half_size - 1, half_size)
+    inner_srcs = (half_size,)
     await_first(inner_srcs)
 
     @pl.when(holds)

time: 50.7 us -> 50.7 us (level)
  no operation moved by 1% of the time
where the time goes in v7:
time: 50.7 us; the launch traced here: 50.1 us
  Pallas kernels  49.1 us (97%)
  local copies, waits for them, and re-layouts  0.97 us (2%)
    pallas_call x1, Pallas kernels, in_one_kernel(): pl.pallas_call(functools.partial(merge_kernel, n, rngs), out_shape=pltpu....  49.1 us

profile of v7, /device:TPU:15, one launch (start us, length us, event | category | flops | bytes accessed | tf_op | source)
XLA Modules:
  0.0 50.1 jit_solution(5770381543739462827)
XLA Ops:
  0.0 49.1 %shard_map.64 = bf16[2,2,128,1024]{3,2,1,0:T(8,128)(2,1)S(1)} custom-call(bf16[2,2,128,1024]{3,2,1,0:T(8,128)(2,1)} %image_hbm.1, bf16[4,2,2,2,128,128]{5,4,3,2,1,0:T(8,128)(2,1)} %weights_hbm.1, f32[4,4]{1,0:T(4,128)} %taps_hbm.1, s32[4,2,128]{2,1,0:T(2,128)} %shifts_hbm.1, f32[3,2,2,64,128]{4,3,2,1,0:T(8,128)} %constant.4.clone.rows_hbm, ...), custom_call_target="tpu_custom_call" | custom-call | tf_op jit(solution)/shard_map/pallas_call | solution.py:629
  49.2 1.0 %copy.8 = bf16[2,2,128,1024]{3,2,1,0:T(8,128)(2,1)} copy(bf16[2,2,128,1024]{3,2,1,0:T(8,128)(2,1)S(1)} %shard_map.64) | data formatting | bytes 2097152

commit v8 on v7

--- a/solution.py
+++ b/solution.py
@@ -166,7 +166,7 @@
 def merge_kernel(
     n, rngs, image_hbm, weights_hbm, taps_hbm, shifts_hbm, rows_hbm, cols_hbm, out,
     image, weights, taps, shifts, rows_table, cols_table, load_sem,
-    raw, xt, big, table, xf, sh0, sh1, sh2, ybuf, stage,
+    raw, xt, rim_out, rim_in, big, table, xf, sh0, sh1, sh2, ybuf, stage,
     tile_send, tile_recv, twin_send, twin_recv, out_send, out_recv,
     rim_send, rim_recv, seen, met,
 ):
@@ -233,10 +233,8 @@
 
     def rim_copy():
         return pltpu.make_async_remote_copy(
-            src_ref=xt.at[:, :, pl.ds(pl.multiple_of(HALO + twin * (block - HALO), HALO), HALO), :],
-            dst_ref=xt.at[
-                :, :, pl.ds(pl.multiple_of((1 - twin) * (block + HALO), HALO), HALO), :
-            ],
+            src_ref=rim_out,
+            dst_ref=rim_in,
             send_sem=rim_send,
             recv_sem=rim_recv,
             device_id={"sub": rim_sub, "rng": rim_rng},
@@ -453,6 +451,8 @@
 
     @pl.when(jnp.logical_not(ends))
     def _():
+        rim = pl.ds(pl.multiple_of(HALO + twin * (block - HALO), HALO), HALO)
+        rim_out[...] = xt[:, :, rim, :].astype(jnp.bfloat16)
         rim_copy().start()
 
     for part in range(max(1, len(parts) - 1), len(parts)):
@@ -462,6 +462,7 @@
     @pl.when(jnp.logical_not(ends))
     def _():
         rim_copy().wait()
+        xt[:, :, halo_at, :] = rim_in[...].astype(jnp.float32)
 
     @pl.when(ends)
     def _():
@@ -641,6 +642,8 @@
             dma((9,)),
             pltpu.VMEM((n, 2, ANGLES, block), bf16),
             pltpu.VMEM((n, 2, block + 2 * HALO + 8, ANGLES), f32),
+            pltpu.VMEM((n, 2, HALO, ANGLES), bf16),
+            pltpu.VMEM((n, 2, HALO, ANGLES), bf16),
             pltpu.VMEM((LEVELS, 4 * ANGLES, 4 * ANGLES), bf16),
             pltpu.VMEM((LEVELS - 1, 2, 2, rows, ANGLES), f32),
             pltpu.VMEM((n, 2, rows + 8, ANGLES), f32),

time: 50.7 us -> 50.7 us (level)
  no operation moved by 1% of the time
where the time goes in v8:
time: 50.7 us; the launch traced here: 49.8 us
  Pallas kernels  48.8 us (96%)
  local copies, waits for them, and re-layouts  0.97 us (2%)
    pallas_call x1, Pallas kernels, in_one_kernel(): pl.pallas_call(functools.partial(merge_kernel, n, rngs), out_shape=pltpu....  48.8 us

profile of v8, /device:TPU:15, one launch (start us, length us, event | category | flops | bytes accessed | tf_op | source)
XLA Modules:
  0.0 49.8 jit_solution(10489103438162513464)
XLA Ops:
  0.0 48.8 %shard_map.64 = bf16[2,2,128,1024]{3,2,1,0:T(8,128)(2,1)S(1)} custom-call(bf16[2,2,128,1024]{3,2,1,0:T(8,128)(2,1)} %image_hbm.1, bf16[4,2,2,2,128,128]{5,4,3,2,1,0:T(8,128)(2,1)} %weights_hbm.1, f32[4,4]{1,0:T(4,128)} %taps_hbm.1, s32[4,2,128]{2,1,0:T(2,128)} %shifts_hbm.1, f32[3,2,2,64,128]{4,3,2,1,0:T(8,128)} %constant.4.clone.rows_hbm, ...), custom_call_target="tpu_custom_call" | custom-call | tf_op jit(solution)/shard_map/pallas_call | solution.py:630
  48.8 1.0 %copy.8 = bf16[2,2,128,1024]{3,2,1,0:T(8,128)(2,1)} copy(bf16[2,2,128,1024]{3,2,1,0:T(8,128)(2,1)S(1)} %shard_map.64) | data formatting | bytes 2097152
